TPU v7x, 128 devices: a whole 4x4x4 slice. The times are simulated.
128 devices in a mesh: dp: 16 (over x, y), tensor: 8 (over z, core).
Axes of the slice: x: 4, y: 4, z: 4, core: 2. Of those that a mesh axis runs over, the one named last changes fastest.
Arguments:
- hidden: bfloat16 [4096, 28672], P('dp', 'tensor'), may hold values from -6 to 6
- hidden_check: bfloat16 [16, 28672], P(None, 'tensor'), may hold values from -96 to 96
- down_weight: bfloat16 [28672, 8192], P('tensor', 'dp'), may hold values from -0.03125 to 0.03125
- weight_check: bfloat16 [28672, 64], P('tensor', 'dp'), may hold values from -0.40039062 to 0.40039062
Outputs:
- output: bfloat16 [4096, 8192], P('tensor', 'dp')
- row_residual: float32 [4096, 64], P('tensor', 'dp')
- col_residual: float32 [8192], P('dp')
All inputs are finite; a program needn't handle non-finite values.
Results may differ from a plain program's by a relative error of at most 0.001.
Values may be sent and summed in bfloat16 or wider, within the bound.
A program may use at most 128 MiB of HBM per device.

v0:
```python
import jax
import jax.numpy as jnp
from jax import lax
from jax.sharding import PartitionSpec as P

CHECK_BLOCK = 128


def side_by_side(arrays, axis, dim, along):
    ends, at = ([], 0)
    for a in arrays[:-1]:
        at += a.shape[along]
        ends.append(at)
    both = jnp.concatenate(arrays, axis=along)
    return tuple(
        jnp.split(lax.psum_scatter(both, axis, scatter_dimension=dim, tiled=True), ends, axis=along)
    )


def shards(hidden, hidden_check, down_weight, weight_check):
    total_rows = hidden.shape[0] * lax.axis_size("dp")
    gathered = lax.all_gather(hidden, "dp", axis=0, tiled=True)
    check_part = jnp.dot(gathered, weight_check, preferred_element_type=jnp.float32)
    check_rows = jnp.dot(hidden_check, down_weight, preferred_element_type=jnp.float32)
    check_sum = check_rows.sum(0)
    partial_value = jnp.dot(gathered, down_weight, preferred_element_type=jnp.float32)
    differ_part = check_part - partial_value.reshape(total_rows, -1, CHECK_BLOCK).sum(-1)
    column_part = partial_value.sum(0)
    column_total = lax.psum(check_sum - column_part, "tensor")
    summed, row_differ = side_by_side((partial_value, differ_part), "tensor", 0, 1)
    output = summed.astype(jnp.bfloat16)
    row_residual = row_differ * CHECK_BLOCK ** (-0.5)
    col_residual = column_total * total_rows ** (-0.5)
    return (output, row_residual, col_residual)


def solution(mesh):
    placed = (P("dp", "tensor"), P(None, "tensor"), P("tensor", "dp"), P("tensor", "dp"))
    return jax.shard_map(
        shards,
        mesh=mesh,
        in_specs=placed,
        out_specs=(P("tensor", "dp"), P("tensor", "dp"), P("dp")),
        check_vma=False,
    )
```

profile of v0, /device:TPU:1, one launch (start us, length us, event | category | flops | bytes accessed | tf_op | source)
XLA Modules:
  0.0 292.3 jit_solution(16352722333425143547)
XLA Ops:
  7.2 0.0 copy-start
  7.2 0.0 all-gather.2.cloned.1.call-start
  7.2 0.7 all-gather.2.cloned.1.call-update
  7.9 0.0 copy-start.2
  7.9 0.0 reduce-scatter.2.cloned.1.call-start
  8.0 180.7 %all-gather.2.cloned.1.call-done = bf16[4096,3584]{1,0:T(8,128)(2,1)} async-done(((bf16[256,3584]{1,0:T(8,128)(2,1)}), bf16[4096,3584]{1,0:T(8,128)(2,1)}) %all-gather.2.cloned.1.call-update) | async-done | bytes 29360144 | tf_op jit(solution)/shard_map/all_gather | solution.py:22
  188.6 20.2 %bitcast_reduce_fusion = (f32[4096,4]{0,1:T(4,128)S(1)}, f32[4096,512]{0,1:T(8,128)S(1)}) fusion(bf16[4096,3584]{1,0:T(8,128)(2,1)} %all-gather.2.cloned.1.call-done, bf16[3584,512]{1,0:T(8,128)(2,1)} %param.6), kind=kOutput, calls=%fused_computation.1 | convolution fusion | flops 15034466304 | bytes 41484288 | tf_op jit(solution)/shard_map/dot_general | solution.py:26
  208.9 0.0 copy-start.1
  208.9 0.0 copy-done.2
  208.9 16.3 %convolution_subtract_fusion = f32[4096,4]{0,1:T(4,128)S(1)} fusion(f32[4096,4]{0,1:T(4,128)S(1)} %get-tuple-element.6, bf16[4096,3584]{1,0:T(8,128)(2,1)} %all-gather.2.cloned.1.call-done, bf16[3584,4]{0,1:T(4,128)(2,1)S(1)} %copy-done.2), kind=kOutput, calls=%fused_computation.2 | convolution fusion | flops 117456896 | bytes 29519872 | tf_op jit(solution)/shard_map/dot_general | solution.py:23
  225.1 0.0 copy-done.1
  225.2 3.9 %pad_maximum_fusion = f32[4096,516]{0,1:T(8,128)} fusion(f32[4096,4]{0,1:T(4,128)S(1)} %convolution_subtract_fusion, f32[4096,512]{0,1:T(8,128)S(1)} %get-tuple-element.7), kind=kLoop, calls=%fused_computation | loop fusion | flops 2113536 | bytes 16908288 | tf_op jit(solution)/shard_map/concatenate | solution.py:14
  229.0 0.0 reduce-scatter.2.cloned.1.call-update
  229.1 0.0 copy-done
  229.1 2.6 convolution_reduce_fusion
  231.7 3.8 %reduce_sum.29 = f32[512]{0:T(512)S(1)} reduce(f32[4096,512]{0,1:T(8,128)} %copy-done.1, f32[]{:T(128)} %constant.0.clone.1), dimensions={0}, to_apply=%region_3.0 | reduce | flops 2096640 | bytes 8390660 | tf_op jit(solution)/shard_map/reduce_sum | solution.py:28
  235.6 12.9 %psum.7 = f32[512]{0:T(512)S(1)} all-reduce(f32[512]{0:T(512)S(1)} %sub.7), channel_id=1, replica_groups=mesh['dp'=16,'tensor'=8] {'tensor'}, use_global_device_ids=true, to_apply=%region_4.0 | all-reduce | flops 512 | bytes 4096 | tf_op jit(solution)/shard_map/psum | solution.py:29
  248.5 0.6 broadcast_multiply_fusion
  249.1 32.7 %reduce-scatter.2.cloned.1.call-done = f32[512,516]{0,1:T(8,128)} async-done(((f32[4096,516]{0,1:T(8,128)}), f32[512,516]{0,1:T(8,128)}) %reduce-scatter.2.cloned.1.call-update) | async-done | bytes 1056784 | tf_op jit(solution)/shard_map/reduce_scatter | solution.py:16
  281.8 1.3 split.13
  283.1 1.0 copy.7
  284.1 1.3 slice_multiply_fusion
  (1 shorter events, 0.0 us)
Async XLA Ops:
  7.2 221.9 %copy-start = (bf16[16,3584]{1,0:T(8,128)(2,1)S(1)}, bf16[16,3584]{1,0:T(8,128)(2,1)}, u32[]{:S(2)}) copy-start(bf16[16,3584]{1,0:T(8,128)(2,1)} %param.5) | copy-start | bytes 344068
  7.2 181.5 %all-gather.2.cloned.1.call-start = ((), (), s32[]{:S(2)}) async-start(), calls=%async_computation.1 | async-start | bytes 31195136 | tf_op jit(solution)/shard_map/all_gather | solution.py:22
  7.9 201.0 %copy-start.2 = (bf16[3584,4]{0,1:T(4,128)(2,1)S(1)}, bf16[3584,4]{0,1:T(4,128)(2,1)}, u32[]{:S(2)}) copy-start(bf16[3584,4]{0,1:T(4,128)(2,1)} %param.7) | copy-start | bytes 86020
  7.9 273.9 %reduce-scatter.2.cloned.1.call-start = ((), (), s32[]{:S(2)}) async-start(), calls=%async_computation.2 | async-start | bytes 9584640 | tf_op jit(solution)/shard_map/reduce_scatter | solution.py:16
  208.9 16.3 %copy-start.1 = (f32[4096,512]{0,1:T(8,128)}, f32[4096,512]{0,1:T(8,128)S(1)}, u32[]{:S(2)}) copy-start(f32[4096,512]{0,1:T(8,128)S(1)} %get-tuple-element.7) | copy-start | bytes 25165828
Sparse Core Ops, SparseCore 0:
  10.2 178.4 all-gather.1
  229.2 52.6 reduce-scatter.1
where the time goes:
time: 293 us; the launch traced here: 292 us
  waiting for transfers between devices  214 us (73%)
  matrix products  39.1 us (13%)
  between operations  14.1 us (5%)
  blocking collectives  12.9 us (4%)
  other arithmetic  9.62 us (3%)
    all_gather x1, waiting for transfers between devices, shards(): gathered = lax.all_gather(hidden, 'dp', axis=0, tiled=True)  181 us
    reduce_scatter x1, waiting for transfers between devices, side_by_side(): lax.psum_scatter(both, axis, scatter_dimension=dim, tiled=True)  32.7 us
    dot_general x1, matrix products, shards(): jnp.dot(gathered, down_weight, preferred_element_type=jnp.float32)  20.2 us
    dot_general x1, matrix products, shards(): jnp.dot(gathered, weight_check, preferred_element_type=jnp.float32)  16.3 us
    psum x1, blocking collectives, shards(): column_total = lax.psum(check_sum - column_part, 'tensor')  12.9 us
  transfers between devices with their start and end apart: 2, of which 2 were waited for; matrix products, arithmetic and copies ran while one was open for 2% of the time, Pallas kernels for 0%

commit v1 on v0

v1 whole, which is shorter than its diff:
```python
import jax
import jax.numpy as jnp
from jax import lax
from jax.experimental import pallas as pl
from jax.experimental.pallas import tpu as pltpu
from jax.sharding import PartitionSpec as P

CHECK_BLOCK = 128
MESH = pl.DeviceIdType.MESH

PIECE = 64
N_PIECE = 4
ROWS = 72
PIECES = 32


def kernel(
    h_hbm,
    hc_ref,
    w_hbm,
    wc_ref,
    out_hbm,
    rr_ref,
    col_ref,
    hbuf,
    wbuf,
    wcpar,
    wct,
    pbuf,
    rbuf,
    zr,
    obuf,
    rrbuf,
    rrpar,
    cbuf,
    cpar,
    vbuf,
    lsem,
    hs,
    hr,
    ws,
    wr,
    ds_s,
    ds_r,
    zs,
    zrs,
    os_s,
    os_r,
    vs,
    vr,
):
    dp = lax.axis_index("dp")
    t = lax.axis_index("tensor")
    x, y = dp // 4, dp % 4
    z, c = t // 2, t % 2
    group = y // 2
    role = (c + group) % 2
    x_next = ((x + 1) % 4) * 4 + y
    x_prev = ((x + 3) % 4) * 4 + y
    y_near = x * 4 + (y // 2) * 2 + (y + 1) % 2
    y_far = x * 4 + 3 - y
    t_other = z * 2 + 1 - c

    def remote(src, dst, send, recv, dev):
        return pltpu.make_async_remote_copy(
            src_ref=src, dst_ref=dst, send_sem=send, recv_sem=recv, device_id=dev, device_id_type=MESH
        )

    h_in = [
        pltpu.make_async_copy(h_hbm.at[pl.ds(PIECE * i, PIECE)], hbuf.at[pl.ds(PIECE * i, PIECE)], lsem.at[i])
        for i in range(N_PIECE)
    ]
    w_in = [
        pltpu.make_async_copy(w_hbm.at[:, pl.ds(256 * j, 256)], wbuf.at[j], lsem.at[N_PIECE + j]) for j in range(2)
    ]
    for copy in h_in + w_in:
        copy.start()

    barrier = pltpu.get_barrier_semaphore()
    peers = [(x_next, t), (x_prev, t), (y_near, t), (y_far, t), (y_far, t_other)]
    peers += [(dp, (t + d) % 8) for d in range(1, 8)]
    for peer in peers:
        pl.semaphore_signal(barrier, inc=1, device_id=peer, device_id_type=MESH)
    pl.semaphore_wait(barrier, len(peers))

    def step_row(s):
        if s < 4:
            return 256 + 192 * s
        if s < 6:
            return 1024 + 128 * (s - 4)
        return 1280 + 192 * (s - 6)

    def h_copy(s, d):
        if s < 4:
            row = PIECE * s
        elif d == 2:
            k = s - 6
            row = step_row(4 + k // 2) + PIECE * (k % 2)
        elif s < 6:
            row = step_row(s - 4) if d == 0 else step_row(s - 2) + PIECE
        else:
            row = step_row(s - 6) + 2 * PIECE
        dev = ((x_next, t), (x_prev, t), (y_near, t))[d]
        return remote(
            hbuf.at[pl.ds(row, PIECE)], hbuf.at[pl.ds(step_row(s) + PIECE * d, PIECE)], hs.at[s, d], hr.at[s, d], dev
        )

    def dirs(s):
        return (0, 1) if s in (4, 5) else (0, 1, 2)

    for i in range(N_PIECE):
        h_in[i].wait()
        for d in dirs(i):
            h_copy(i, d).start()
    wc_copy = remote(wc_ref, wcpar, ws.at[2], wr.at[2], (y_far, t))
    wc_copy.start()
    w_copy = [remote(wbuf.at[j], wbuf.at[2 + j], ws.at[j], wr.at[j], (y_far, t)) for j in range(2)]
    for j in range(2):
        w_in[j].wait()
        w_copy[j].start()

    def give(j, p):
        @pl.when(j // 2 != role)
        def _():
            remote(
                pbuf.at[j, p], rbuf.at[j % 2, p], ds_s.at[j % 2, p], ds_r.at[j % 2, p], (dp, t_other)
            ).start()

    def mm(row, m, piece, j):
        out = jnp.dot(hbuf[pl.ds(row, m), :], wbuf[j], preferred_element_type=jnp.float32)
        for i in range(m // PIECE):
            pbuf[j, piece + i, 0:PIECE, :] = out[PIECE * i : PIECE * (i + 1)]
        for i in range(m // PIECE):
            give(j, piece + i)

    def checks(row, m, piece):
        out = lax.dot_general(
            hbuf[pl.ds(row, m), :], wct[...], (((1,), (1,)), ((), ())), preferred_element_type=jnp.float32
        )
        for i in range(m // PIECE):
            turned = out[PIECE * i : PIECE * (i + 1)].T
            pbuf[0, piece + i, PIECE:ROWS, 0:PIECE] = turned[0:8]
            pbuf[2, piece + i, PIECE:ROWS, 0:PIECE] = turned[16:24]

    def compute(row, m, piece, n_j):
        checks(row, m, piece)

        @pl.loop(0, n_j)
        def _(j):
            mm(row, m, piece, j)

    def add_up(half, p, zd, q):
        remote(pbuf.at[0, p], rbuf.at[half, p], ds_s.at[half, p], ds_r.at[half, p], (dp, t_other)).wait_recv()
        total = pbuf[2 * role + half, p] + rbuf[half, p]

        @pl.when(zd == z)
        def _():
            zr[z, half, q] = total

        @pl.when(zd != z)
        def _():
            pbuf[2 * role + half, p] = total
            remote(
                pbuf.at[2 * role + half, p],
                zr.at[z, half, q],
                zs.at[half, p],
                zrs.at[z, half, q],
                (dp, zd * 2 + c),
            ).start()

    q_own = (y % 2) * 4
    q_near = ((y + 1) % 2) * 4

    def own_dest(i):
        return i, x, q_own + i

    def a_dest(s, d):
        return 4 + 3 * s + d, (x + (3, 1, 0)[d]) % 4, (q_own, q_own, q_near)[d] + s

    def b_dest(s, d):
        return 16 + 2 * s + d, (x + 2) % 4, q_own + s + 2 * d

    def c_dest(s, d):
        place = s if d < 2 else s // 2 + 2 * (s % 2)
        return 20 + 3 * s + d, (x + (3, 1, 2)[d]) % 4, q_near + place

    def add_own(half):
        @pl.loop(0, 4)
        def _(i):
            p, zd, q = own_dest(i)
            add_up(half, p, zd, q)

    def add_step(dest, n_d, s, half):
        for d in range(n_d):
            p, zd, q = dest(s, d)
            add_up(half, p, zd, q)

    wct[...] = jnp.zeros_like(wct)
    wct[0:4, :] = wc_ref[...]
    wc_copy.wait_recv()
    wct[16:20, :] = wcpar[...]

    compute(0, 256, 0, 2)

    @pl.when(role == 0)
    def _():
        @pl.loop(0, 2)
        def _(half):
            add_own(half)

    for half in range(2):
        rows = jnp.dot(hc_ref[...], wbuf[half], preferred_element_type=jnp.float32)
        cbuf[:, 256 * half : 256 * (half + 1)] = rows[0:8] + rows[8:16]

    def arrive(s):
        for d in dirs(s):
            h_copy(s, d).wait_recv()
        if 4 <= s + 2 < 10:
            for d in dirs(s + 2):
                h_copy(s + 2, d).start()

    def both(n_half, dest, n_d, s):
        @pl.when(role == 0)
        def _():
            @pl.loop(0, 2)
            def _(half):
                add_step(dest, n_d, s, half)

        if n_half:

            @pl.when(role == 1)
            def _():
                @pl.loop(0, n_half)
                def _(half):
                    add_step(dest, n_d, s, half)

    for s in range(10):
        arrive(s)
        if s < 4:
            compute(step_row(s), 192, 4 + 3 * s, 2)
            both(0, a_dest, 3, s)
        elif s < 6:
            compute(step_row(s), 128, 16 + 2 * (s - 4), 3)
            both(1, b_dest, 2, s - 4)
        else:
            compute(step_row(s), 192, 20 + 3 * (s - 6), 3 if s < 8 else 4)
            both(1 if s < 8 else 2, c_dest, 3, s - 6)
        if s == 3:
            w_copy[0].wait_recv()

            @pl.loop(0, 4)
            def _(i):
                mm(256 * i, 256, 4 * i, 2)

            @pl.when(role == 1)
            def _():
                add_own(0)

                @pl.loop(0, 4)
                def _(k):
                    add_step(a_dest, 3, k, 0)

        if s == 7:
            w_copy[1].wait_recv()

            @pl.loop(0, 13)
            def _(i):
                mm(128 * i, 128, 2 * i, 3)

            @pl.when(role == 1)
            def _():
                add_own(1)

                @pl.loop(0, 4)
                def _(k):
                    add_step(a_dest, 3, k, 1)

                @pl.loop(0, 2)
                def _(k):
                    add_step(b_dest, 2, k, 1)
                    add_step(c_dest, 3, k, 1)

    lane = lax.broadcasted_iota(jnp.int32, (PIECE, 128), 1)
    vbuf[t] = jnp.zeros_like(vbuf[t])

    @pl.loop(0, 8)
    def _(q):
        for d in range(1, 4):
            for half in range(2):
                zf = (z + d) % 4
                remote(
                    pbuf.at[0, 0], zr.at[zf, half, q], zs.at[0, 0], zrs.at[zf, half, q], (dp, zf * 2 + c)
                ).wait_recv()
        marks = jnp.zeros((PIECE, 128), jnp.float32)
        for half in range(2):
            full = (zr[0, half, q, 0:PIECE, :] + zr[1, half, q, 0:PIECE, :]) + (
                zr[2, half, q, 0:PIECE, :] + zr[3, half, q, 0:PIECE, :]
            )
            obuf[pl.ds(q * PIECE, PIECE), 256 * half : 256 * (half + 1)] = full.astype(jnp.bfloat16)
            vbuf[t, :, 256 * half : 256 * (half + 1)] += full.reshape(8, 8, 256).sum(0)
            for b in range(2):
                sums = full[:, 128 * b : 128 * (b + 1)].sum(-1, keepdims=True)
                marks = jnp.where(lane == 2 * half + b, sums, marks)
        check = (zr[0, 0, q, PIECE:ROWS, 0:PIECE] + zr[1, 0, q, PIECE:ROWS, 0:PIECE]) + (
            zr[2, 0, q, PIECE:ROWS, 0:PIECE] + zr[3, 0, q, PIECE:ROWS, 0:PIECE]
        )
        rrbuf[q, :, 0:PIECE] = (check - marks.T[0:8]) * CHECK_BLOCK ** (-0.5)

    partner = (y_far, t_other)
    out_far = remote(obuf, out_hbm, os_s.at[0], os_r.at[0], partner)
    rr_far = remote(rrbuf, rrpar, os_s.at[1], os_r.at[1], partner)
    col_far = remote(vbuf.at[t], cpar, os_s.at[2], os_r.at[2], partner)
    out_near = pltpu.make_async_copy(obuf, out_hbm, lsem.at[6])

    def write_rows(src):
        for q in range(8):
            rr_ref[:, PIECE * q : PIECE * (q + 1)] = src[q, 0:4, 0:PIECE]

    @pl.when(role == 0)
    def _():
        out_near.start()
        vbuf[t] = cbuf[...] - vbuf[t]
        write_rows(rrbuf)

    @pl.when(role == 1)
    def _():
        col_far.start()
        rr_far.start()
        out_far.start()
        col_far.wait()
        vbuf[t] = cbuf[...] - cpar[...]

    for d in range(1, 8):
        remote(vbuf.at[t], vbuf.at[t], vs.at[d - 1], vr.at[t], (dp, (t + d) % 8)).start()

    @pl.when(role == 0)
    def _():
        out_near.wait()

    @pl.when(role == 1)
    def _():
        rr_far.wait()
        write_rows(rrpar)
        out_far.wait()

    for d in range(1, 8):
        src = (t + d) % 8
        remote(vbuf.at[src], vbuf.at[src], vs.at[d - 1], vr.at[src], (dp, src)).wait_recv()
    total = vbuf[0]
    for i in range(1, 8):
        total = total + vbuf[i]
    col_ref[...] = total.sum(0, keepdims=True) * 4096 ** (-0.5)

    for d in range(1, 8):
        remote(vbuf.at[t], vbuf.at[t], vs.at[d - 1], vr.at[t], (dp, (t + d) % 8)).wait_send()
    for s in range(10):
        for d in dirs(s):
            h_copy(s, d).wait_send()
    wc_copy.wait_send()
    for j in range(2):
        w_copy[j].wait_send()

    @pl.loop(0, 2)
    def _(half):
        @pl.loop(0, PIECES)
        def _(p):
            remote(
                pbuf.at[0, p], rbuf.at[half, p], ds_s.at[half, p], ds_r.at[half, p], (dp, t_other)
            ).wait_send()

        def sent(p, zd):
            @pl.when(zd != z)
            def _():
                remote(pbuf.at[0, p], zr.at[0, half, 0], zs.at[half, p], zrs.at[z, half, 0], (dp, t_other)).wait_send()

        for i in range(4):
            sent(*own_dest(i)[:2])
            for d in range(3):
                sent(*a_dest(i, d)[:2])
                sent(*c_dest(i, d)[:2])
        for i in range(2):
            for d in range(2):
                sent(*b_dest(i, d)[:2])


def shards(hidden, hidden_check, down_weight, weight_check):
    f32, bf16 = jnp.float32, jnp.bfloat16
    k = hidden.shape[1]
    dma = pltpu.SemaphoreType.DMA
    out, rr, col = pl.pallas_call(
        kernel,
        out_shape=(
            jax.ShapeDtypeStruct((512, 512), bf16),
            jax.ShapeDtypeStruct((4, 512), f32),
            jax.ShapeDtypeStruct((1, 512), f32),
        ),
        in_specs=[
            pl.BlockSpec(memory_space=pl.ANY),
            pl.BlockSpec(memory_space=pltpu.VMEM),
            pl.BlockSpec(memory_space=pl.ANY),
            pl.BlockSpec(memory_space=pltpu.VMEM),
        ],
        out_specs=(
            pl.BlockSpec(memory_space=pl.ANY),
            pl.BlockSpec(memory_space=pltpu.VMEM),
            pl.BlockSpec(memory_space=pltpu.VMEM),
        ),
        scratch_shapes=[
            pltpu.VMEM((2048, k), bf16),
            pltpu.VMEM((4, k, 256), bf16),
            pltpu.VMEM((4, k), bf16),
            pltpu.VMEM((128, k), bf16),
            pltpu.VMEM((4, PIECES, ROWS, 256), f32),
            pltpu.VMEM((2, PIECES, ROWS, 256), f32),
            pltpu.VMEM((4, 2, 8, ROWS, 256), f32),
            pltpu.VMEM((512, 512), bf16),
            pltpu.VMEM((8, 8, 128), f32),
            pltpu.VMEM((8, 8, 128), f32),
            pltpu.VMEM((8, 512), f32),
            pltpu.VMEM((8, 512), f32),
            pltpu.VMEM((8, 8, 512), f32),
            dma((7,)),
            dma((10, 3)),
            dma((10, 3)),
            dma((3,)),
            dma((3,)),
            dma((2, PIECES)),
            dma((2, PIECES)),
            dma((2, PIECES)),
            dma((4, 2, 8)),
            dma((3,)),
            dma((3,)),
            dma((7,)),
            dma((8,)),
        ],
        compiler_params=pltpu.CompilerParams(
            collective_id=0, has_side_effects=True, vmem_limit_bytes=60 * 1024 * 1024
        ),
    )(hidden, hidden_check, down_weight, weight_check.T)
    return out, rr.T, col.reshape(512)


def solution(mesh):
    placed = (P("dp", "tensor"), P(None, "tensor"), P("tensor", "dp"), P("tensor", "dp"))
    return jax.shard_map(
        shards,
        mesh=mesh,
        in_specs=placed,
        out_specs=(P("tensor", "dp"), P("tensor", "dp"), P("dp")),
        check_vma=False,
    )
```

time: 293 us -> 142 us (0.48)
  waiting for transfers between devices: 214 us -> 0 us
  Pallas kernels: 0 us -> 136 us
  matrix products: 39.1 us -> 0 us
  between operations: 14.1 us -> 0.64 us
  blocking collectives: 12.9 us -> 0 us
  other arithmetic: 9.62 us -> 0 us
    all_gather x1 -> x0, waiting for transfers between devices: 181 us -> none  [shards(): gathered = lax.all_gather(hidden, 'dp', axis=0, tiled=True)]
    pallas_call x0 -> x1, Pallas kernels: none -> 136 us  [shards(): pl.pallas_call(kernel, out_shape=(jax.ShapeDtypeStruct((512, 512), bf16),...]
    dot_general x3 -> x0, matrix products: 39.1 us -> none  [the longest x1 20.2 us: shards(): jnp.dot(gathered, down_weight, preferred_element_type=jnp.float32)]
    reduce_scatter x1 -> x0, waiting for transfers between devices: 32.7 us -> none  [side_by_side(): lax.psum_scatter(both, axis, scatter_dimension=dim, tiled=True)]
    psum x1 -> x0, blocking collectives: 12.9 us -> none  [shards(): column_total = lax.psum(check_sum - column_part, 'tensor')]
    concatenate x1 -> x0, other arithmetic: 3.86 us -> none  [side_by_side(): both = jnp.concatenate(arrays, axis=along)]
    reduce_sum x1 -> x0, other arithmetic: 3.85 us -> none  [shards(): column_part = partial_value.sum(0)]
    unnamed x7 -> x3, local copies, waits for them, and re-layouts: 1.03 us -> 4.41 us
  transfers between devices with their start and end apart: 2 -> 0, of which waited for: 2 -> 0; matrix products, arithmetic and copies ran while one was open for 2% -> 0% of each run, Pallas kernels for 0% -> 0%
where the time goes in v1:
time: 142 us; the launch traced here: 141 us
  Pallas kernels  136 us (96%)
  local copies, waits for them, and re-layouts  4.41 us (3%)
    pallas_call x1, Pallas kernels, shards(): pl.pallas_call(kernel, out_shape=(jax.ShapeDtypeStruct((512, 512), bf16),...  136 us
    unnamed x3, local copies, waits for them, and re-layouts  4.41 us

profile of v1, /device:TPU:1, one launch (start us, length us, event | category | flops | bytes accessed | tf_op | source)
XLA Modules:
  0.0 141.2 jit_solution(6166340854216565121)
XLA Ops:
  0.6 136.1 %shard_map.67 = (bf16[512,512]{1,0:T(8,128)(2,1)}, f32[4,512]{1,0:T(4,128)}, f32[1,512]{1,0:T(1,128)}) custom-call(bf16[256,3584]{1,0:T(8,128)(2,1)} %h_hbm.1, bf16[16,3584]{1,0:T(8,128)(2,1)} %hc_ref.1, bf16[3584,512]{1,0:T(8,128)(2,1)} %w_hbm.1, bf16[4,3584]{1,0:T(4,128)(2,1)} %bitcast.3), custom_call_target="tpu_custom_call" | custom-call | tf_op jit(solution)/shard_map/pallas_call | solution.py:390
  136.7 1.9 %copy.10 = bf16[512,512]{1,0:T(8,128)(2,1)} copy(bf16[512,512]{1,0:T(8,128)(2,1)} %get-tuple-element.12) | data formatting | bytes 1048576
  138.6 1.3 copy.11
  139.9 1.2 copy.12

commit v2 on v0

v2 whole, which is shorter than its diff:
```python
import jax
import jax.numpy as jnp
from jax import lax
from jax.experimental import pallas as pl
from jax.experimental.pallas import tpu as pltpu
from jax.sharding import PartitionSpec as P

CHECK_BLOCK = 128
MESH = pl.DeviceIdType.MESH

PIECE = 32
OWN = 8
STEPS = 19
PIECES = 64
ROWS = (40, 32)


def kernel(
    h_hbm, hc_hbm, w_hbm, wc_hbm,
    out_hbm, rr_ref, col_ref,
    hbuf, wbuf, hcbuf, wcown, wcpar, wct, wck, pbuf, rbuf, rl, zr, obuf, rrbuf, rrt, rrpar, cbuf, cpar, vbuf,
    lsem, osem, hs, hr, ws, wr, ds_s, ds_r, zs, zrs, rls, os_s, os_r, fs, fr, vs, vr,
):
    f32, bf16 = jnp.float32, jnp.bfloat16
    dp = lax.axis_index("dp")
    t = lax.axis_index("tensor")
    x, y = dp // 4, dp % 4
    z, c = t // 2, t % 2
    group = y // 2
    role = (c + group) % 2
    x_next = ((x + 1) % 4) * 4 + y
    x_prev = ((x + 3) % 4) * 4 + y
    y_near = x * 4 + (y // 2) * 2 + (y + 1) % 2
    y_far = x * 4 + 3 - y
    t_other = z * 2 + 1 - c
    partner = (y_far, t_other)

    def remote(src, dst, send, recv, dev):
        return pltpu.make_async_remote_copy(
            src_ref=src, dst_ref=dst, send_sem=send, recv_sem=recv, device_id=dev, device_id_type=MESH
        )

    h_in = pltpu.make_async_copy(h_hbm, hbuf.at[pl.ds(0, PIECE * OWN)], lsem.at[0])
    w_in = [pltpu.make_async_copy(w_hbm.at[:, pl.ds(256 * j, 256)], wbuf.at[j], lsem.at[1 + j]) for j in range(2)]
    hc_in = pltpu.make_async_copy(hc_hbm, hcbuf, lsem.at[3])
    wc_in = pltpu.make_async_copy(wc_hbm, wcown, lsem.at[4])
    h_in.start()
    wc_in.start()
    w_in[0].start()
    w_in[1].start()
    hc_in.start()

    barrier = pltpu.get_barrier_semaphore()
    peers = [(x_next, t), (x_prev, t), (y_near, t), (y_far, t), partner]
    peers += [(dp, (t + d) % 8) for d in range(1, 8)]
    for peer in peers:
        pl.semaphore_signal(barrier, inc=1, device_id=peer, device_id_type=MESH)
    pl.semaphore_wait(barrier, len(peers))

    def piece(s, d):
        return OWN + 3 * s + d

    def source(s, d):
        if s < 8:
            return s
        if d == 2:
            if s < 10:
                return piece(0, s - 8)
            return piece(8 + (s - 10) // 2, (s - 10) % 2)
        if s < 12:
            return piece(s - 8, 0) if d == 0 else piece(s - 4, 1)
        return piece(s - 11, 2)

    def dirs(s):
        return range(3) if s < STEPS - 1 else range(2)

    def h_copy(s, d):
        dev = ((x_next, t), (x_prev, t), (y_near, t))[d]
        return remote(
            hbuf.at[pl.ds(PIECE * source(s, d), PIECE)],
            hbuf.at[pl.ds(PIECE * piece(s, d), PIECE)],
            hs.at[s, d],
            hr.at[s, d],
            dev,
        )

    h_in.wait()
    for s in range(OWN):
        for d in dirs(s):
            h_copy(s, d).start()
    wc_in.wait()
    wc_copy = remote(wcown, wcpar, ws.at[2], wr.at[2], (y_far, t))
    wc_copy.start()
    w_copy = [remote(wbuf.at[j], wbuf.at[2 + j], ws.at[j], wr.at[j], (y_far, t)) for j in range(2)]
    for j in range(2):
        w_in[j].wait()
        w_copy[j].start()

    def core_copy(j, half, p):
        rows = pl.ds(0, ROWS[half])
        return remote(
            pbuf.at[j, p, rows], rbuf.at[half, p, rows], ds_s.at[half, p], ds_r.at[half, p], (dp, t_other)
        )

    def mm(row, m, p, j):
        out = jnp.dot(hbuf[pl.ds(row, m), :], wbuf[j], preferred_element_type=f32)
        for i in range(m // PIECE):
            pbuf[j, p + i, 0:PIECE, :] = out[PIECE * i : PIECE * (i + 1)]
        for half in range(2):

            @pl.when(j == 2 * (1 - role) + half)
            def _():
                for i in range(m // PIECE):
                    core_copy(j, half, p + i).start()

    def checks(row, m, p):
        out = jnp.dot(hbuf[pl.ds(row, m), :], wck[...], preferred_element_type=f32)
        for i in range(m // PIECE):
            turned = out[PIECE * i : PIECE * (i + 1)].T
            pbuf[0, p + i, PIECE : PIECE + 8, 0:PIECE] = turned[0:8]
            pbuf[2, p + i, PIECE : PIECE + 8, 0:PIECE] = turned[16:24]

    def compute(p, n_p, n_j):
        checks(PIECE * p, PIECE * n_p, p)

        @pl.loop(0, n_j)
        def _(i):
            j = (i + 2 * (1 - role)) % 4 if n_j == 4 else i
            mm(PIECE * p, PIECE * n_p, p, j)

    def add_up(half, p, zd, q):
        rows = pl.ds(0, ROWS[half])
        j = 2 * role + half
        core_copy(j, half, p).wait_recv()
        total = pbuf[j, p, 0 : ROWS[half]] + rbuf[half, p, 0 : ROWS[half]]
        away = (zd - z + 4) % 4

        @pl.when(away == 0)
        def _():
            zr[0, half, q, 0 : ROWS[half]] = total

        @pl.when(away != 0)
        def _():
            pbuf[j, p, 0 : ROWS[half]] = total

        @pl.when(away == 2)
        def _():
            to = (z + (1, 3)[half]) % 4
            remote(
                pbuf.at[j, p, rows], rl.at[half, q, rows], zs.at[half, p], rls.at[half, q], (dp, to * 2 + c)
            ).start()

        @pl.when(away == (3, 1)[half])
        def _():
            remote(
                pbuf.at[j, p, rows],
                zr.at[2 - half, half, q, rows],
                zs.at[half, p],
                zrs.at[1 - half, half, q],
                (dp, zd * 2 + c),
            ).start()

    def pass_on(half, p, zd, q):
        rows = pl.ds(0, ROWS[half])
        j = 2 * role + half

        @pl.when((zd - z + 4) % 4 == (1, 3)[half])
        def _():
            remote(pbuf.at[j, p, rows], rl.at[half, q, rows], zs.at[half, p], rls.at[half, q], (dp, t_other)).wait_recv()
            pbuf[j, p, 0 : ROWS[half]] += rl[half, q, 0 : ROWS[half]]
            remote(
                pbuf.at[j, p, rows],
                zr.at[1 + half, half, q, rows],
                zs.at[half, p],
                zrs.at[half, half, q],
                (dp, zd * 2 + c),
            ).start()

    q_own = (y % 2) * OWN
    q_near = ((y + 1) % 2) * OWN

    def own_dest(i):
        return i, x, q_own + i

    def early_dest(s, d):
        return piece(s, d), (x + (3, 1, 0)[d]) % 4, (q_own, q_own, q_near)[d] + s

    def late_dest(s, d):
        if d == 2:
            if s < 10:
                return piece(s, d), (x + (3, 1)[s - 8]) % 4, q_near
            k = s - 10
            return piece(s, d), (x + 2) % 4, q_near + k // 2 + 4 * (k % 2)
        if s < 12:
            return piece(s, d), (x + 2) % 4, q_own + s - (8, 4)[d]
        return piece(s, d), (x + (3, 1)[d]) % 4, q_near + s - 11

    def own_items(half):
        def run(act):
            @pl.loop(0, OWN)
            def _(i):
                act(half, *own_dest(i))

        return run

    def early_items(low, high, half):
        def run(act):
            @pl.loop(low, high)
            def _(s):
                for d in range(3):
                    act(half, *early_dest(s, d))

        return run

    def late_items(low, high, half):
        def run(act):
            for s in range(low, high):
                for d in dirs(s):
                    act(half, *late_dest(s, d))

        return run

    waiting = [[], []]

    def relay():
        for r in range(2):
            if waiting[r]:

                @pl.when(role == r)
                def _():
                    for run in waiting[r]:
                        run(pass_on)

                waiting[r] = []

    def collect(r, items):
        @pl.when(role == r)
        def _():
            for run in items:
                run(add_up)

        waiting[r] += items

    wct[...] = jnp.zeros_like(wct)
    wct[0:4, :] = wcown[...]
    wc_copy.wait_recv()
    wct[16:20, :] = wcpar[...]

    @pl.loop(0, wct.shape[1] // 128)
    def _(i):
        part = pl.ds(pl.multiple_of(i * 128, 128), 128)
        wck[part, :] = wct[:, part].astype(f32).T.astype(bf16)

    compute(0, OWN, 2)
    collect(0, [own_items(half) for half in range(2)])

    hc_in.wait()
    for half in range(2):
        rows = jnp.dot(hcbuf[...], wbuf[half], preferred_element_type=f32)
        cbuf[:, 256 * half : 256 * (half + 1)] = rows[0:8] + rows[8:16]
    vbuf[t] = jnp.zeros_like(vbuf[t])

    def arrive(s):
        for d in dirs(s):
            h_copy(s, d).wait_recv()
        if OWN <= s + 2 < STEPS:
            for d in dirs(s + 2):
                h_copy(s + 2, d).start()

    lane = lax.broadcasted_iota(jnp.int32, (PIECE, 128), 1)

    def out_copies(q):
        rows = pl.ds(PIECE * q, PIECE)
        near = pltpu.make_async_copy(obuf.at[rows], out_hbm.at[rows], osem.at[q])
        far = remote(obuf.at[rows], out_hbm.at[rows], os_s.at[q], os_r.at[q], partner)
        return near, far

    def finish(q):
        for half in range(2):
            rows = pl.ds(0, ROWS[half])
            for side in range(2):
                remote(
                    pbuf.at[0, 0, rows],
                    zr.at[1 + side, half, q, rows],
                    zs.at[0, 0],
                    zrs.at[side, half, q],
                    (dp, t_other),
                ).wait_recv()
        marks = jnp.zeros((PIECE, 128), f32)
        for half in range(2):
            full = zr[0, half, q, 0:PIECE, :] + (zr[1, half, q, 0:PIECE, :] + zr[2, half, q, 0:PIECE, :])
            obuf[pl.ds(q * PIECE, PIECE), 256 * half : 256 * (half + 1)] = full.astype(bf16)
            vbuf[t, :, 256 * half : 256 * (half + 1)] += full.reshape(PIECE // 8, 8, 256).sum(0)
            for b in range(2):
                sums = full[:, 128 * b : 128 * (b + 1)].sum(-1, keepdims=True)
                marks = jnp.where(lane == 2 * half + b, sums, marks)
        near, far = out_copies(q)

        @pl.when(role == 0)
        def _():
            near.start()

        @pl.when(role == 1)
        def _():
            far.start()

        check = zr[0, 0, q, PIECE : PIECE + 8, 0:PIECE] + (
            zr[1, 0, q, PIECE : PIECE + 8, 0:PIECE] + zr[2, 0, q, PIECE : PIECE + 8, 0:PIECE]
        )
        rrbuf[q, :, 0:PIECE] = (check - marks.T[0:8]) * CHECK_BLOCK ** (-0.5)

    for low, high in ((0, 2), (2, 4), (4, 6), (6, 8), (8, 10), (10, 12), (12, 14), (14, 16), (16, 17), (17, 18), (18, 19)):
        for s in range(low, high):
            arrive(s)
        relay()
        n_j = 2 if low < 8 else 3 if low < 16 else 4
        compute(piece(low, 0), sum(len(dirs(s)) for s in range(low, high)), n_j)
        items = early_items if low < 8 else late_items
        collect(0, [items(low, high, half) for half in range(2)])
        if n_j > 2:
            collect(1, [items(low, high, half) for half in range(n_j - 2)])
        if high in (8, 16):
            half = high // 8 - 1
            w_copy[half].wait_recv()

            @pl.loop(0, (OWN + 3 * high) // 8)
            def _(i):
                mm(256 * i, 256, 8 * i, 2 + half)

            caught = [own_items(half), early_items(0, 8, half)]
            if half:
                caught.append(late_items(8, high, half))
            collect(1, caught)
        if high == STEPS - 1:

            @pl.loop(0, OWN)
            def _(i):
                finish(q_own + i)

            for few in ((0, 3), (4, 5)):

                @pl.loop(*few)
                def _(i):
                    finish(q_near + i)

    relay()
    for few in ((3, 4), (5, 8)):

        @pl.loop(*few)
        def _(i):
            finish(q_near + i)

    rr_far = remote(rrt, rrpar, fs.at[0], fr.at[0], partner)
    col_far = remote(vbuf.at[t], cpar, fs.at[1], fr.at[1], partner)

    @pl.when(role == 0)
    def _():
        vbuf[t] = cbuf[...] - vbuf[t]

    @pl.when(role == 1)
    def _():
        col_far.start()

    for q in range(2 * OWN):
        rrt[:, PIECE * q : PIECE * (q + 1)] = rrbuf[q, :, 0:PIECE]

    @pl.when(role == 1)
    def _():
        rr_far.start()
        col_far.wait()
        vbuf[t] = cbuf[...] - cpar[...]

    for d in range(1, 8):
        remote(vbuf.at[t], vbuf.at[t], vs.at[d - 1], vr.at[t], (dp, (t + d) % 8)).start()

    for s in range(STEPS):
        for d in dirs(s):
            h_copy(s, d).wait_send()
    wc_copy.wait_send()
    for j in range(2):
        w_copy[j].wait_send()

    @pl.loop(0, PIECES)
    def _(p):
        for half in range(2):
            core_copy(0, half, p).wait_send()

    def sent(half, p, zd, q):
        rows = pl.ds(0, ROWS[half])

        @pl.when(zd != z)
        def _():
            remote(
                pbuf.at[0, p, rows], zr.at[0, half, 0, rows], zs.at[half, p], zrs.at[0, half, 0], (dp, t_other)
            ).wait_send()

    for half in range(2):
        own_items(half)(sent)
        early_items(0, 8, half)(sent)
        late_items(8, STEPS, half)(sent)

    @pl.when(role == 0)
    def _():
        rr_ref[...] = rrt[0:4]

        @pl.loop(0, 2 * OWN)
        def _(q):
            out_copies(q)[0].wait()

    @pl.when(role == 1)
    def _():
        rr_far.wait()
        rr_ref[...] = rrpar[0:4]

        @pl.loop(0, 2 * OWN)
        def _(q):
            out_copies(q)[1].wait()

    for d in range(1, 8):
        src = (t + d) % 8
        remote(vbuf.at[src], vbuf.at[src], vs.at[d - 1], vr.at[src], (dp, src)).wait_recv()
    total = vbuf[0]
    for i in range(1, 8):
        total = total + vbuf[i]
    col_ref[...] = total.sum(0, keepdims=True) * 4096 ** (-0.5)
    for d in range(1, 8):
        remote(vbuf.at[t], vbuf.at[t], vs.at[d - 1], vr.at[t], (dp, (t + d) % 8)).wait_send()


def hand_over(out_in, rr_in, col_in, out_ref, rr_ref, col_ref):
    out_ref[...] = out_in[...]
    rr_ref[...] = rr_in[...]
    col_ref[...] = col_in[...]


def shards(hidden, hidden_check, down_weight, weight_check):
    f32, bf16 = jnp.float32, jnp.bfloat16
    k = hidden.shape[1]
    dma = pltpu.SemaphoreType.DMA
    shapes = (
        jax.ShapeDtypeStruct((512, 512), bf16),
        jax.ShapeDtypeStruct((4, 512), f32),
        jax.ShapeDtypeStruct((1, 512), f32),
    )
    vmem = pl.BlockSpec(memory_space=pltpu.VMEM)
    whole = pl.BlockSpec(memory_space=pl.ANY)
    results = pl.pallas_call(
        kernel,
        out_shape=shapes,
        in_specs=[whole] * 4,
        out_specs=(whole, vmem, vmem),
        scratch_shapes=[
            pltpu.VMEM((PIECE * PIECES, k), bf16),
            pltpu.VMEM((4, k, 256), bf16),
            pltpu.VMEM((16, k), bf16),
            pltpu.VMEM((4, k), bf16),
            pltpu.VMEM((4, k), bf16),
            pltpu.VMEM((128, k), bf16),
            pltpu.VMEM((k, 128), bf16),
            pltpu.VMEM((4, PIECES, 40, 256), f32),
            pltpu.VMEM((2, PIECES, 40, 256), f32),
            pltpu.VMEM((2, 16, 40, 256), f32),
            pltpu.VMEM((3, 2, 16, 40, 256), f32),
            pltpu.VMEM((512, 512), bf16),
            pltpu.VMEM((16, 8, 128), f32),
            pltpu.VMEM((8, 512), f32),
            pltpu.VMEM((8, 512), f32),
            pltpu.VMEM((8, 512), f32),
            pltpu.VMEM((8, 512), f32),
            pltpu.VMEM((8, 8, 512), f32),
            dma((5,)),
            dma((16,)),
            dma((STEPS, 3)),
            dma((STEPS, 3)),
            dma((3,)),
            dma((3,)),
            dma((2, PIECES)),
            dma((2, PIECES)),
            dma((2, PIECES)),
            dma((2, 2, 16)),
            dma((2, 16)),
            dma((16,)),
            dma((16,)),
            dma((2,)),
            dma((2,)),
            dma((7,)),
            dma((8,)),
        ],
        compiler_params=pltpu.CompilerParams(
            collective_id=0, has_side_effects=True, vmem_limit_bytes=60 * 1024 * 1024
        ),
    )(hidden, hidden_check, down_weight, weight_check.T)
    out, rr, col = pl.pallas_call(hand_over, out_shape=shapes, in_specs=[vmem] * 3, out_specs=(vmem,) * 3)(*results)
    return out, rr.T, col.reshape(512)


def solution(mesh):
    placed = (P("dp", "tensor"), P(None, "tensor"), P("tensor", "dp"), P("tensor", "dp"))
    return jax.shard_map(
        shards,
        mesh=mesh,
        in_specs=placed,
        out_specs=(P("tensor", "dp"), P("tensor", "dp"), P("dp")),
        check_vma=False,
    )
```

time: 293 us -> 145 us (0.49)
  waiting for transfers between devices: 214 us -> 0 us
  Pallas kernels: 0 us -> 144 us
  matrix products: 39.1 us -> 0 us
  between operations: 14.1 us -> 0.64 us
  blocking collectives: 12.9 us -> 0 us
  other arithmetic: 9.62 us -> 0 us
    all_gather x1 -> x0, waiting for transfers between devices: 181 us -> none  [shards(): gathered = lax.all_gather(hidden, 'dp', axis=0, tiled=True)]
    pallas_call x0 -> x2, Pallas kernels: none -> 144 us  [the longest x1 142 us: shards(): pl.pallas_call(kernel, out_shape=shapes, in_specs=[whole] * 4, out_specs=...]
    dot_general x3 -> x0, matrix products: 39.1 us -> none  [the longest x1 20.2 us: shards(): jnp.dot(gathered, down_weight, preferred_element_type=jnp.float32)]
    reduce_scatter x1 -> x0, waiting for transfers between devices: 32.7 us -> none  [side_by_side(): lax.psum_scatter(both, axis, scatter_dimension=dim, tiled=True)]
    psum x1 -> x0, blocking collectives: 12.9 us -> none  [shards(): column_total = lax.psum(check_sum - column_part, 'tensor')]
    concatenate x1 -> x0, other arithmetic: 3.86 us -> none  [side_by_side(): both = jnp.concatenate(arrays, axis=along)]
    reduce_sum x1 -> x0, other arithmetic: 3.85 us -> none  [shards(): column_part = partial_value.sum(0)]
  transfers between devices with their start and end apart: 2 -> 0, of which waited for: 2 -> 0; matrix products, arithmetic and copies ran while one was open for 2% -> 0% of each run, Pallas kernels for 0% -> 0%
where the time goes in v2:
time: 145 us
  Pallas kernels  144 us (99%)
    pallas_call x1, Pallas kernels, shards(): pl.pallas_call(kernel, out_shape=shapes, in_specs=[whole] * 4, out_specs=...  142 us

profile of v2, /device:TPU:1, one launch (start us, length us, event | category | flops | bytes accessed | tf_op | source)
XLA Modules:
  0.0 144.8 jit_solution(16179472565608483409)
XLA Ops:
  0.6 142.3 %shard_map.67 = (bf16[512,512]{1,0:T(8,128)(2,1)}, f32[4,512]{1,0:T(4,128)}, f32[1,512]{1,0:T(1,128)}) custom-call(bf16[256,3584]{1,0:T(8,128)(2,1)} %h_hbm.1, bf16[16,3584]{1,0:T(8,128)(2,1)} %hc_hbm.1, bf16[3584,512]{1,0:T(8,128)(2,1)} %w_hbm.1, bf16[4,3584]{1,0:T(4,128)(2,1)} %bitcast.3), custom_call_target="tpu_custom_call" | custom-call | tf_op jit(solution)/shard_map/pallas_call | solution.py:447
  142.9 1.9 %shard_map.68 = (bf16[512,512]{1,0:T(8,128)(2,1)}, f32[4,512]{1,0:T(4,128)}, f32[1,512]{1,0:T(1,128)}) custom-call(bf16[512,512]{1,0:T(8,128)(2,1)} %get-tuple-element.9.out_in, f32[4,512]{1,0:T(4,128)} %get-tuple-element.10.rr_in, f32[1,512]{1,0:T(1,128)} %get-tuple-element.11.col_in), custom_call_target="tpu_custom_call" | custom-call | tf_op jit(solution)/shard_map/pallas_call | solution.py:493

commit v3 on v0

v3 whole, which is shorter than its diff:
```python
import jax
import jax.numpy as jnp
from jax import lax
from jax.experimental import pallas as pl
from jax.experimental.pallas import tpu as pltpu
from jax.sharding import PartitionSpec as P

CHECK_BLOCK = 128
MESH = pl.DeviceIdType.MESH

PIECE = 32
OWN = 8
STEPS = 19
AHEAD = 4
BLOCK = 64
SLOTS = 34


def kernel(
    h_hbm, hc_hbm, w_hbm, wc_hbm,
    out_hbm, rr_ref, col_ref,
    hbuf, wbuf, hcbuf, wcown, wcpar, wct, wck, pbuf, rbuf, rl, zr, obuf, rrbuf, rrpart, rrt, rrpar, cbuf, colsum, nbuf, fbuf,
    lsem, osem, hs, hr, ws, wr, ds_s, ds_r, zs, zrs, rls, os_s, os_r, fs, fr, cs, cr, vs, vr,
):
    f32, bf16 = jnp.float32, jnp.bfloat16
    dp = lax.axis_index("dp")
    t = lax.axis_index("tensor")
    x, y = dp // 4, dp % 4
    z, c = t // 2, t % 2
    group = y // 2
    role = (c + group) % 2
    x_next = ((x + 1) % 4) * 4 + y
    x_prev = ((x + 3) % 4) * 4 + y
    y_near = x * 4 + (y // 2) * 2 + (y + 1) % 2
    y_far = x * 4 + 3 - y
    t_other = z * 2 + 1 - c
    partner = (y_far, t_other)

    def remote(src, dst, send, recv, dev):
        return pltpu.make_async_remote_copy(
            src_ref=src, dst_ref=dst, send_sem=send, recv_sem=recv, device_id=dev, device_id_type=MESH
        )

    h_in = pltpu.make_async_copy(h_hbm, hbuf.at[pl.ds(0, PIECE * OWN)], lsem.at[0])
    w_in = [pltpu.make_async_copy(w_hbm.at[:, pl.ds(256 * j, 256)], wbuf.at[j], lsem.at[1 + j]) for j in range(2)]
    hc_in = pltpu.make_async_copy(hc_hbm, hcbuf, lsem.at[3])
    wc_in = pltpu.make_async_copy(wc_hbm, wcown, lsem.at[4])
    h_in.start()
    wc_in.start()
    w_in[0].start()
    w_in[1].start()
    hc_in.start()

    barrier = pltpu.get_barrier_semaphore()
    peers = [(x_next, t), (x_prev, t), (y_near, t)]
    peers += [(dp, (t + d) % 8) for d in range(1, 8)]
    peers += [(y_far, (t + d) % 8) for d in range(8)]
    for peer in peers:
        pl.semaphore_signal(barrier, inc=1, device_id=peer, device_id_type=MESH)
    pl.semaphore_wait(barrier, len(peers))

    def row_of(s, d):
        if s is None:
            return PIECE * d
        if s == STEPS - 1:
            return PIECE * (OWN + 54 + d)
        return PIECE * (OWN + 6 * (s // 2) + 2 * d + s % 2)

    def source(s, d):
        if s < 8:
            return None, s
        if d == 2:
            if s < 10:
                return 0, s - 8
            k = (0, 1, 4, 5, 2, 3, 6, 7)[s - 10]
            return 8 + k % 4, k // 4
        if s < 12:
            return (s - 8, 0) if d == 0 else (s - 4, 1)
        return s - 11, 2

    def dirs(s):
        return range(3) if s < STEPS - 1 else range(2)

    def h_copy(s, d):
        dev = ((x_next, t), (x_prev, t), (y_near, t))[d]
        return remote(
            hbuf.at[pl.ds(row_of(*source(s, d)), PIECE)],
            hbuf.at[pl.ds(row_of(s, d), PIECE)],
            hs.at[s, d],
            hr.at[s, d],
            dev,
        )

    h_in.wait()
    for s in range(OWN):
        for d in dirs(s):
            h_copy(s, d).start()
    wc_in.wait()
    wc_copy = remote(wcown, wcpar, ws.at[2], wr.at[2], (y_far, t))
    wc_copy.start()
    w_copy = [remote(wbuf.at[j], wbuf.at[2 + j], ws.at[j], wr.at[j], (y_far, t)) for j in range(2)]
    for j in range(2):
        w_in[j].wait()
        w_copy[j].start()

    def core_copy(half, slot, rows, j=0):
        rows = pl.ds(0, rows)
        return remote(
            pbuf.at[j, slot, rows], rbuf.at[half, slot, rows], ds_s.at[half, slot], ds_r.at[half, slot], (dp, t_other)
        )

    def slot_of(pair, d):
        return 4 + 9 * d + pair

    def pair_slots(pair):
        if isinstance(pair, int) and pair == 4:
            return [(slot_of(4, 0), BLOCK), (slot_of(4, 1), BLOCK), (26, PIECE), (31, PIECE)]
        return [(slot_of(pair, d), BLOCK) for d in range(3)]

    own_slots = [(i, BLOCK) for i in range(4)]
    last_slots = [(32, PIECE), (33, PIECE)]

    def mm(row, slots, j):
        m = sum(n for _, n in slots)
        out = jnp.dot(hbuf[pl.ds(row, m), :], wbuf[j], preferred_element_type=f32)
        at = 0
        for slot, n in slots:
            pbuf[j, slot, 0:n, :] = out[at : at + n]
            at += n
        for half in range(2):

            @pl.when(j == 2 * (1 - role) + half)
            def _():
                for slot, n in slots:
                    core_copy(half, slot, n + 8, j).start()

    def checks(row, slots):
        m = sum(n for _, n in slots)
        out = jnp.dot(hbuf[pl.ds(row, m), :], wck[...], preferred_element_type=f32)
        at = 0
        for slot, n in slots:
            turned = out[at : at + n].T
            pbuf[0, slot, n : n + 8, 0:n] = turned[0:8]
            pbuf[2, slot, n : n + 8, 0:n] = turned[16:24]
            at += n

    def compute(row, slots, n_j):
        checks(row, slots)

        @pl.loop(0, n_j)
        def _(i):
            j = (i + 2 * (1 - role)) % 4 if n_j == 4 else i
            mm(row, slots, j)

    def parts(item):
        (h0, nh), (slot, ns), n, zd, q, way = item
        return (pl.ds(h0, nh), pl.ds(q, ns), pl.ds(0, n + 8)), (zd - z + 4) % 4

    def each(item):
        (h0, nh), (slot, ns), n, zd, q, way = item
        for half in range(h0, h0 + nh):
            for i in range(ns):
                yield half, slot + i, q + i, n + 8

    def send_to(r, item, dst, recv, to):
        (h0, nh), (slot, ns), n, zd, q, way = item
        src = pbuf.at[pl.ds(2 * r + h0, nh), pl.ds(slot, ns), pl.ds(0, n + 8)]
        return remote(src, dst, zs.at[h0, slot], recv, (dp, to * 2 + c))

    def to_relay(r, item):
        (h0, nh), (slot, ns), n, zd, q, way = item
        at, _ = parts(item)
        return send_to(r, item, rl.at[(way,) + at], rls.at[way, h0, q], (z + 1 + 2 * way) % 4)

    def to_owner(r, item, side):
        (h0, nh), (slot, ns), n, zd, q, way = item
        at, _ = parts(item)
        return send_to(r, item, zr.at[(1 + side,) + at], zrs.at[side, h0, q], zd)

    def add_up(r, item):
        for half, slot, q, rows in each(item):
            core_copy(half, slot, rows).wait_recv()
        way = item[-1]
        _, away = parts(item)

        @pl.when(away == 0)
        def _():
            for half, slot, q, rows in each(item):
                zr[0, half, q, 0:rows] = pbuf[2 * r + half, slot, 0:rows] + rbuf[half, slot, 0:rows]

        @pl.when(away != 0)
        def _():
            for half, slot, q, rows in each(item):
                pbuf[2 * r + half, slot, 0:rows] += rbuf[half, slot, 0:rows]

        @pl.when(away == 2)
        def _():
            to_relay(r, item).start()

        @pl.when(away == 3 - 2 * way)
        def _():
            to_owner(r, item, 1 - way).start()

    def pass_on(r, item):
        way = item[-1]
        _, away = parts(item)

        @pl.when(away == 1 + 2 * way)
        def _():
            to_relay(r, item).wait_recv()
            for half, slot, q, rows in each(item):
                pbuf[2 * r + half, slot, 0:rows] += rl[way, half, q, 0:rows]
            to_owner(r, item, way).start()

    def take(r, item):
        _, away = parts(item)

        @pl.when(away == 0)
        def _():
            for side in range(2):
                to_owner(r, item, side).wait_recv()

    def sent(r, item):
        _, away = parts(item)

        @pl.when(away != 0)
        def _():
            to_owner(r, item, 0).wait_send()

    def own_items(halves):
        def run(act):
            for i in (0, 2):
                act((halves, (i, 2), BLOCK, x, i, i // 2))

        return run

    def early_items(halves, low, n):
        def run(act):
            @pl.loop(0, 3)
            def _(d):
                for pair in range(low, low + 4 if n == 2 else low + 1, n):
                    zd = (x + 3 - 2 * d + d // 2) % 4
                    act((halves, (slot_of(pair, d), n), BLOCK, zd, pair + 4 * (d // 2), pair // 2))

        return run

    def late_items(halves, pair):
        def run(act):
            @pl.loop(0, 2)
            def _(d):
                if pair < 6:
                    act((halves, (slot_of(pair, d), 1), BLOCK, (x + 2) % 4, pair - 4 + 2 * d, pair % 2))
                else:
                    act((halves, (slot_of(pair, d), 1), BLOCK, (x + 3 - 2 * d + 4) % 4, pair - 1, pair % 2))

            if pair == 4:
                act((halves, (26, 1), PIECE, (x + 3) % 4, 4, 0))
                act((halves, (31, 1), PIECE, (x + 1) % 4, 4, 1))
            else:
                q = (4, 6, 5, 7)[pair - 5]
                act((halves, (slot_of(pair, 2), 1), BLOCK, (x + 2) % 4, q, (pair + 1) % 2))

        return run

    def last_items(halves):
        def run(act):
            @pl.loop(0, 2)
            def _(d):
                act((halves, (32 + d, 1), PIECE, (x + 3 - 2 * d) % 4, 8, 1))

        return run

    waiting = [[], []]
    gone = [[], []]

    def over(r, items, act):
        @pl.when(role == r)
        def _():
            for run in items:
                run(lambda item: act(r, item))

    def relay():
        for r in range(2):
            if waiting[r]:
                over(r, waiting[r], pass_on)
                gone[r] += waiting[r]
                waiting[r] = []

    def collect(r, items):
        over(r, items, add_up)
        waiting[r] += items

    wct[...] = jnp.zeros_like(wct)
    wct[0:4, :] = wcown[...]
    wc_copy.wait_recv()
    wct[16:20, :] = wcpar[...]

    @pl.loop(0, wct.shape[1] // 128)
    def _(i):
        part = pl.ds(pl.multiple_of(i * 128, 128), 128)
        wck[part, :] = wct[:, part].astype(f32).T.astype(bf16)

    both, first, second = (0, 2), (0, 1), (1, 1)
    compute(0, own_slots, 2)
    collect(0, [own_items(both)])

    hc_in.wait()
    for half in range(2):
        rows = jnp.dot(hcbuf[...], wbuf[half], preferred_element_type=f32)
        cbuf[t, :, 256 * half : 256 * (half + 1)] = rows[0:8] + rows[8:16]
    check_copies = [
        remote(cbuf.at[t], cbuf.at[t], cs.at[d - 1], cr.at[t], (dp, (t + d) % 8)) for d in range(1, 8)
    ]
    for copy in check_copies:
        copy.start()
    colsum[...] = jnp.zeros_like(colsum)

    def arrive(s):
        for d in dirs(s):
            h_copy(s, d).wait_recv()
        for later in range(OWN, STEPS):
            for d in dirs(later):
                if max(later - AHEAD, source(later, d)[0]) == s:
                    h_copy(later, d).start()

    def out_copies(q, row, n):
        rows = pl.ds(pl.multiple_of(row, PIECE), n)
        near = pltpu.make_async_copy(obuf.at[rows], out_hbm.at[rows], osem.at[q])
        far = remote(obuf.at[rows], out_hbm.at[rows], os_s.at[q], os_r.at[q], partner)
        return near, far

    def finish(q, row, n):
        lane = lax.broadcasted_iota(jnp.int32, (n, 128), 1)
        marks = jnp.zeros((n, 128), f32)
        for half in range(2):
            full = zr[0, half, q, 0:n, :] + (zr[1, half, q, 0:n, :] + zr[2, half, q, 0:n, :])
            obuf[pl.ds(pl.multiple_of(row, PIECE), n), 256 * half : 256 * (half + 1)] = full.astype(bf16)
            colsum[:, 256 * half : 256 * (half + 1)] += full.reshape(n // 8, 8, 256).sum(0)
            for b in range(2):
                sums = full[:, 128 * b : 128 * (b + 1)].sum(-1, keepdims=True)
                marks = jnp.where(lane == 2 * half + b, sums, marks)
        near, far = out_copies(q, row, n)

        @pl.when(role == 0)
        def _():
            near.start()

        @pl.when(role == 1)
        def _():
            far.start()

        check = zr[0, 0, q, n : n + 8, 0:n] + (zr[1, 0, q, n : n + 8, 0:n] + zr[2, 0, q, n : n + 8, 0:n])
        rrbuf[q, :, 0:n] = (check - marks.T[0:8]) * CHECK_BLOCK ** (-0.5)

    row_own = (y % 2) * 256
    row_near = ((y + 1) % 2) * 256
    apart = (z - x + 4) % 2

    def finish_near(act, late):
        @pl.when(apart == 0)
        def _():
            @pl.loop(7 if late else 4, 8 if late else 7)
            def _(q):
                act(q, row_near + BLOCK * (q - 4), BLOCK)

        @pl.when(apart == 1)
        def _():
            act(8 if late else 4, row_near + (224 if late else 0), PIECE)

            @pl.loop(7 if late else 5, 8 if late else 7)
            def _(q):
                act(q, row_near + PIECE + BLOCK * (q - 5), BLOCK)

    def finish_own(act):
        @pl.loop(0, 4)
        def _(q):
            act(q, row_own + BLOCK * q, BLOCK)

    def catch_up(pairs, half):
        w_copy[half].wait_recv()
        mm(0, own_slots, 2 + half)
        for low, high in pairs:
            if high - low == 1:
                mm(row_of(2 * low, 0), pair_slots(low), 2 + half)
            else:

                @pl.loop(low, high)
                def _(pair):
                    mm(PIECE * OWN + 192 * pair, pair_slots(pair), 2 + half)

    for pair in range(9):
        arrive(2 * pair)
        arrive(2 * pair + 1)
        relay()
        compute(row_of(2 * pair, 0), pair_slots(pair), 2 if pair < 4 else 3 if pair < 8 else 4)
        if pair < 4:
            if pair == 3:
                catch_up([(0, 4)], 0)
            collect(0, [early_items(both, pair, 1)])
            if pair == 3:
                collect(1, [own_items(first), early_items(first, 0, 2)])
        else:
            if pair == 7:
                catch_up([(0, 4), (4, 5), (5, 8)], 1)
            collect(0, [late_items(both, pair)])
            collect(1, [late_items(first if pair < 8 else both, pair)])
            if pair == 7:
                collect(1, [own_items(second), early_items(second, 0, 2)] + [late_items(second, k) for k in range(4, 8)])
                relay()

    early_gone = [list(items) for items in gone]
    for r in range(2):
        over(r, early_gone[r], take)
    finish_own(finish)
    finish_near(finish, False)
    relay()
    arrive(18)
    compute(row_of(18, 0), last_slots, 4)
    for r in range(2):
        collect(r, [last_items(both)])
    relay()
    for r in range(2):
        over(r, gone[r][len(early_gone[r]) :], take)
    finish_near(finish, True)

    near_copies = [remote(colsum, nbuf.at[z], vs.at[d], vr.at[z], (dp, (t + d) % 8)) for d in range(1, 8)]
    far_copies = [remote(colsum, fbuf.at[z], vs.at[d], vr.at[4 + z], (y_far, (t + d) % 8)) for d in range(8)]
    rr_far = remote(rrt, rrpar, fs.at[0], fr.at[0], partner)

    @pl.when(role == 0)
    def _():
        for copy in near_copies:
            copy.start()
        nbuf[z] = colsum[...]

    @pl.when(role == 1)
    def _():
        for copy in far_copies:
            copy.start()

    for q in range(4):
        rrpart[0, :, BLOCK * q : BLOCK * (q + 1)] = rrbuf[q, :, 0:BLOCK]

    @pl.when(apart == 0)
    def _():
        for q in range(4):
            rrpart[1, :, BLOCK * q : BLOCK * (q + 1)] = rrbuf[4 + q, :, 0:BLOCK]

    @pl.when(apart == 1)
    def _():
        rrpart[1, :, 0:PIECE] = rrbuf[4, :, 0:PIECE]
        for q in range(3):
            rrpart[1, :, PIECE + BLOCK * q : PIECE + BLOCK * (q + 1)] = rrbuf[5 + q, :, 0:BLOCK]
        rrpart[1, :, 256 - PIECE : 256] = rrbuf[8, :, 0:PIECE]

    rrt[:, pl.ds(pl.multiple_of(row_own, 256), 256)] = rrpart[0]
    rrt[:, pl.ds(pl.multiple_of(row_near, 256), 256)] = rrpart[1]

    @pl.when(role == 0)
    def _():
        rr_ref[...] = rrt[0:4]

    @pl.when(role == 1)
    def _():
        rr_far.start()

    for s in range(STEPS):
        for d in dirs(s):
            h_copy(s, d).wait_send()
    wc_copy.wait_send()
    for j in range(2):
        w_copy[j].wait_send()
    for copy in check_copies:
        copy.wait_send()
    def given(slot, n):
        for half in range(2):
            core_copy(half, slot, n + 8).wait_send()

    @pl.loop(0, 26)
    def _(slot):
        given(slot, BLOCK)

    @pl.loop(27, 31)
    def _(slot):
        given(slot, BLOCK)

    for slot in (26, 31, 32, 33):
        given(slot, PIECE)
    for r in range(2):
        over(r, gone[r], sent)

    def written(side):
        def act(q, row, n):
            out_copies(q, row, n)[side].wait()

        finish_own(act)
        for late in (False, True):
            finish_near(act, late)

    total = cbuf[t]
    for d in range(1, 8):
        src = (t + d) % 8
        remote(cbuf.at[src], cbuf.at[src], cs.at[d - 1], cr.at[src], (dp, src)).wait_recv()
        total = total + cbuf[src]

    @pl.when(role == 0)
    def _():
        for d in range(1, 4):
            src = (z + d) % 4
            remote(colsum, nbuf.at[src], vs.at[0], vr.at[src], (dp, t_other)).wait_recv()

    @pl.when(role == 1)
    def _():
        for src in range(4):
            remote(colsum, nbuf.at[src], vs.at[0], vr.at[src], (dp, t_other)).wait_recv()

    for src in range(4):
        remote(colsum, fbuf.at[src], vs.at[0], vr.at[4 + src], partner).wait_recv()
    sums = (nbuf[0] + nbuf[1]) + (nbuf[2] + nbuf[3])
    sums = sums + ((fbuf[0] + fbuf[1]) + (fbuf[2] + fbuf[3]))
    col_ref[...] = (total - sums).sum(0, keepdims=True) * 4096 ** (-0.5)

    @pl.when(role == 0)
    def _():
        written(0)

        for copy in near_copies:
            copy.wait_send()

    @pl.when(role == 1)
    def _():
        rr_far.wait()
        rr_ref[...] = rrpar[0:4]

        written(1)

        for copy in far_copies:
            copy.wait_send()


def hand_over(out_in, rr_in, col_in, out_ref, rr_ref, col_ref):
    out_ref[...] = out_in[...]
    rr_ref[...] = rr_in[...]
    col_ref[...] = col_in[...]


def shards(hidden, hidden_check, down_weight, weight_check):
    f32, bf16 = jnp.float32, jnp.bfloat16
    k = hidden.shape[1]
    dma = pltpu.SemaphoreType.DMA
    shapes = (
        jax.ShapeDtypeStruct((512, 512), bf16),
        jax.ShapeDtypeStruct((4, 512), f32),
        jax.ShapeDtypeStruct((1, 512), f32),
    )
    vmem = pl.BlockSpec(memory_space=pltpu.VMEM)
    whole = pl.BlockSpec(memory_space=pl.ANY)
    results = pl.pallas_call(
        kernel,
        out_shape=shapes,
        in_specs=[whole] * 4,
        out_specs=(whole, vmem, vmem),
        scratch_shapes=[
            pltpu.VMEM((2048, k), bf16),
            pltpu.VMEM((4, k, 256), bf16),
            pltpu.VMEM((16, k), bf16),
            pltpu.VMEM((4, k), bf16),
            pltpu.VMEM((4, k), bf16),
            pltpu.VMEM((128, k), bf16),
            pltpu.VMEM((k, 128), bf16),
            pltpu.VMEM((4, SLOTS, BLOCK + 8, 256), f32),
            pltpu.VMEM((2, SLOTS, BLOCK + 8, 256), f32),
            pltpu.VMEM((2, 2, 9, BLOCK + 8, 256), f32),
            pltpu.VMEM((3, 2, 9, BLOCK + 8, 256), f32),
            pltpu.VMEM((512, 512), bf16),
            pltpu.VMEM((9, 8, 128), f32),
            pltpu.VMEM((2, 8, 256), f32),
            pltpu.VMEM((8, 512), f32),
            pltpu.VMEM((8, 512), f32),
            pltpu.VMEM((8, 8, 512), f32),
            pltpu.VMEM((8, 512), f32),
            pltpu.VMEM((4, 8, 512), f32),
            pltpu.VMEM((4, 8, 512), f32),
            dma((5,)),
            dma((9,)),
            dma((STEPS, 3)),
            dma((STEPS, 3)),
            dma((3,)),
            dma((3,)),
            dma((2, SLOTS)),
            dma((2, SLOTS)),
            dma((2, SLOTS)),
            dma((2, 2, 9)),
            dma((2, 2, 9)),
            dma((9,)),
            dma((9,)),
            dma((1,)),
            dma((1,)),
            dma((7,)),
            dma((8,)),
            dma((8,)),
            dma((8,)),
        ],
        compiler_params=pltpu.CompilerParams(
            collective_id=0, has_side_effects=True, vmem_limit_bytes=60 * 1024 * 1024
        ),
    )(hidden, hidden_check, down_weight, weight_check.T)
    out, rr, col = pl.pallas_call(hand_over, out_shape=shapes, in_specs=[vmem] * 3, out_specs=(vmem,) * 3)(*results)
    return out, rr.T, col.reshape(512)


def solution(mesh):
    placed = (P("dp", "tensor"), P(None, "tensor"), P("tensor", "dp"), P("tensor", "dp"))
    return jax.shard_map(
        shards,
        mesh=mesh,
        in_specs=placed,
        out_specs=(P("tensor", "dp"), P("tensor", "dp"), P("dp")),
        check_vma=False,
    )
```

time: 293 us -> 142 us (0.48)
  waiting for transfers between devices: 214 us -> 0 us
  Pallas kernels: 0 us -> 141 us
  matrix products: 39.1 us -> 0 us
  between operations: 14.1 us -> 0.64 us
  blocking collectives: 12.9 us -> 0 us
  other arithmetic: 9.62 us -> 0 us
    all_gather x1 -> x0, waiting for transfers between devices: 181 us -> none  [shards(): gathered = lax.all_gather(hidden, 'dp', axis=0, tiled=True)]
    pallas_call x0 -> x2, Pallas kernels: none -> 141 us  [the longest x1 139 us: shards(): pl.pallas_call(kernel, out_shape=shapes, in_specs=[whole] * 4, out_specs=...]
    dot_general x3 -> x0, matrix products: 39.1 us -> none  [the longest x1 20.2 us: shards(): jnp.dot(gathered, down_weight, preferred_element_type=jnp.float32)]
    reduce_scatter x1 -> x0, waiting for transfers between devices: 32.7 us -> none  [side_by_side(): lax.psum_scatter(both, axis, scatter_dimension=dim, tiled=True)]
    psum x1 -> x0, blocking collectives: 12.9 us -> none  [shards(): column_total = lax.psum(check_sum - column_part, 'tensor')]
    concatenate x1 -> x0, other arithmetic: 3.86 us -> none  [side_by_side(): both = jnp.concatenate(arrays, axis=along)]
    reduce_sum x1 -> x0, other arithmetic: 3.85 us -> none  [shards(): column_part = partial_value.sum(0)]
  transfers between devices with their start and end apart: 2 -> 0, of which waited for: 2 -> 0; matrix products, arithmetic and copies ran while one was open for 2% -> 0% of each run, Pallas kernels for 0% -> 0%
where the time goes in v3:
time: 142 us
  Pallas kernels  141 us (99%)
    pallas_call x1, Pallas kernels, shards(): pl.pallas_call(kernel, out_shape=shapes, in_specs=[whole] * 4, out_specs=...  139 us

profile of v3, /device:TPU:1, one launch (start us, length us, event | category | flops | bytes accessed | tf_op | source)
XLA Modules:
  0.0 141.7 jit_solution(14575659109854457479)
XLA Ops:
  0.6 139.2 %shard_map.67 = (bf16[512,512]{1,0:T(8,128)(2,1)}, f32[4,512]{1,0:T(4,128)}, f32[1,512]{1,0:T(1,128)}) custom-call(bf16[256,3584]{1,0:T(8,128)(2,1)} %h_hbm.1, bf16[16,3584]{1,0:T(8,128)(2,1)} %hc_hbm.1, bf16[3584,512]{1,0:T(8,128)(2,1)} %w_hbm.1, bf16[4,3584]{1,0:T(4,128)(2,1)} %bitcast.3), custom_call_target="tpu_custom_call" | custom-call | tf_op jit(solution)/shard_map/pallas_call | solution.py:558
  139.8 1.9 %shard_map.68 = (bf16[512,512]{1,0:T(8,128)(2,1)}, f32[4,512]{1,0:T(4,128)}, f32[1,512]{1,0:T(1,128)}) custom-call(bf16[512,512]{1,0:T(8,128)(2,1)} %get-tuple-element.9.out_in, f32[4,512]{1,0:T(4,128)} %get-tuple-element.10.rr_in, f32[1,512]{1,0:T(1,128)} %get-tuple-element.11.col_in), custom_call_target="tpu_custom_call" | custom-call | tf_op jit(solution)/shard_map/pallas_call | solution.py:608

commit v4 on v3

--- a/solution.py
+++ b/solution.py
@@ -19,8 +19,8 @@
 def kernel(
     h_hbm, hc_hbm, w_hbm, wc_hbm,
     out_hbm, rr_ref, col_ref,
-    hbuf, wbuf, hcbuf, wcown, wcpar, wct, wck, pbuf, rbuf, rl, zr, obuf, rrbuf, rrpart, rrt, rrpar, cbuf, colsum, nbuf, fbuf,
-    lsem, osem, hs, hr, ws, wr, ds_s, ds_r, zs, zrs, rls, os_s, os_r, fs, fr, cs, cr, vs, vr,
+    hbuf, wbuf, hcbuf, wcown, wcpar, wct, wck, pbuf, rbuf, zr, obuf, rrbuf, rrpart, rrt, rrpar, cbuf, colsum, nbuf, fbuf,
+    lsem, osem, hs, hr, ws, wr, ds_s, ds_r, zs, zrs, os_s, os_r, fs, fr, cs, cr, vs, vr,
 ):
     f32, bf16 = jnp.float32, jnp.bfloat16
     dp = lax.axis_index("dp")
@@ -98,15 +98,25 @@
     wc_in.wait()
     wc_copy = remote(wcown, wcpar, ws.at[2], wr.at[2], (y_far, t))
     wc_copy.start()
-    w_copy = [remote(wbuf.at[j], wbuf.at[2 + j], ws.at[j], wr.at[j], (y_far, t)) for j in range(2)]
-    for j in range(2):
-        w_in[j].wait()
-        w_copy[j].start()
-
-    def core_copy(half, slot, rows, j=0):
-        rows = pl.ds(0, rows)
+    lows, highs = pl.ds(0, 128), pl.ds(128, 128)
+    w_copy = [
+        remote(wbuf.at[0], wbuf.at[2], ws.at[0], wr.at[0], (y_far, t)),
+        remote(wbuf.at[1, :, lows], wbuf.at[3, :, lows], ws.at[1], wr.at[1], (y_far, t)),
+        remote(wbuf.at[1, :, highs], wbuf.at[3, :, highs], ws.at[3], wr.at[3], (y_far, t)),
+    ]
+    for copy in w_in:
+        copy.wait()
+    for copy in w_copy:
+        copy.start()
+
+    both, first = (0, 2, 0, 256, 0), (0, 1, 0, 256, 0)
+    third, fourth = (1, 1, 0, 128, 1), (1, 1, 128, 128, 2)
+
+    def core_copy(half, slot, rows, j=0, lane=0, lanes=256):
+        tag = half + lane // 128
+        at = (slot, pl.ds(0, rows), pl.ds(lane, lanes))
         return remote(
-            pbuf.at[j, slot, rows], rbuf.at[half, slot, rows], ds_s.at[half, slot], ds_r.at[half, slot], (dp, t_other)
+            pbuf.at[(j,) + at], rbuf.at[(half,) + at], ds_s.at[tag, slot], ds_r.at[tag, slot], (dp, t_other)
         )
 
     def slot_of(pair, d):
@@ -119,6 +129,20 @@
 
     own_slots = [(i, BLOCK) for i in range(4)]
     last_slots = [(32, PIECE), (33, PIECE)]
+
+    def mm_part(row, slots, part):
+        half, _, lane, lanes, _ = part
+        m = sum(n for _, n in slots)
+        out = jnp.dot(hbuf[pl.ds(row, m), :], wbuf[3, :, lane : lane + lanes], preferred_element_type=f32)
+        at = 0
+        for slot, n in slots:
+            pbuf[3, slot, 0:n, lane : lane + lanes] = out[at : at + n]
+            at += n
+
+        @pl.when(role == 0)
+        def _():
+            for slot, n in slots:
+                core_copy(1, slot, n, 3, lane, lanes).start()
 
     def mm(row, slots, j):
         m = sum(n for _, n in slots)
@@ -152,85 +176,57 @@
             j = (i + 2 * (1 - role)) % 4 if n_j == 4 else i
             mm(row, slots, j)
 
-    def parts(item):
-        (h0, nh), (slot, ns), n, zd, q, way = item
-        return (pl.ds(h0, nh), pl.ds(q, ns), pl.ds(0, n + 8)), (zd - z + 4) % 4
+    def rows_of(item):
+        return item[2] + (8 if item[0][0] == 0 else 0)
+
+    def away(item):
+        return (item[3] - z + 4) % 4
 
     def each(item):
-        (h0, nh), (slot, ns), n, zd, q, way = item
+        (h0, nh, lane, lanes, tag), (slot, ns), n, zd, q = item
+        cols = slice(lane, lane + lanes)
         for half in range(h0, h0 + nh):
             for i in range(ns):
-                yield half, slot + i, q + i, n + 8
-
-    def send_to(r, item, dst, recv, to):
-        (h0, nh), (slot, ns), n, zd, q, way = item
-        src = pbuf.at[pl.ds(2 * r + h0, nh), pl.ds(slot, ns), pl.ds(0, n + 8)]
-        return remote(src, dst, zs.at[h0, slot], recv, (dp, to * 2 + c))
-
-    def to_relay(r, item):
-        (h0, nh), (slot, ns), n, zd, q, way = item
-        at, _ = parts(item)
-        return send_to(r, item, rl.at[(way,) + at], rls.at[way, h0, q], (z + 1 + 2 * way) % 4)
+                yield half, slot + i, q + i, rows_of(item), cols
 
     def to_owner(r, item, side):
-        (h0, nh), (slot, ns), n, zd, q, way = item
-        at, _ = parts(item)
-        return send_to(r, item, zr.at[(1 + side,) + at], zrs.at[side, h0, q], zd)
+        (h0, nh, lane, lanes, tag), (slot, ns), n, zd, q = item
+        tail = (pl.ds(0, rows_of(item)), pl.ds(lane, lanes))
+        src = pbuf.at[(pl.ds(2 * r + h0, nh), pl.ds(slot, ns)) + tail]
+        dst = zr.at[(1 + side, pl.ds(h0, nh), pl.ds(q, ns)) + tail]
+        return remote(src, dst, zs.at[tag, slot], zrs.at[side, tag, q], (dp, zd * 2 + c))
 
     def add_up(r, item):
-        for half, slot, q, rows in each(item):
-            core_copy(half, slot, rows).wait_recv()
-        way = item[-1]
-        _, away = parts(item)
-
-        @pl.when(away == 0)
-        def _():
-            for half, slot, q, rows in each(item):
-                zr[0, half, q, 0:rows] = pbuf[2 * r + half, slot, 0:rows] + rbuf[half, slot, 0:rows]
-
-        @pl.when(away != 0)
-        def _():
-            for half, slot, q, rows in each(item):
-                pbuf[2 * r + half, slot, 0:rows] += rbuf[half, slot, 0:rows]
-
-        @pl.when(away == 2)
-        def _():
-            to_relay(r, item).start()
-
-        @pl.when(away == 3 - 2 * way)
-        def _():
-            to_owner(r, item, 1 - way).start()
-
-    def pass_on(r, item):
-        way = item[-1]
-        _, away = parts(item)
-
-        @pl.when(away == 1 + 2 * way)
-        def _():
-            to_relay(r, item).wait_recv()
-            for half, slot, q, rows in each(item):
-                pbuf[2 * r + half, slot, 0:rows] += rl[way, half, q, 0:rows]
-            to_owner(r, item, way).start()
+        lane, lanes = item[0][2:4]
+        for half, slot, q, rows, cols in each(item):
+            core_copy(half, slot, rows if lanes == 128 else item[2] + 8, 0, lane, lanes).wait_recv()
+
+        @pl.when(away(item) == 0)
+        def _():
+            for half, slot, q, rows, cols in each(item):
+                zr[0, half, q, 0:rows, cols] = pbuf[2 * r + half, slot, 0:rows, cols] + rbuf[half, slot, 0:rows, cols]
+
+        @pl.when(away(item) != 0)
+        def _():
+            for half, slot, q, rows, cols in each(item):
+                pbuf[2 * r + half, slot, 0:rows, cols] += rbuf[half, slot, 0:rows, cols]
+            to_owner(r, item, away(item) - 1).start()
 
     def take(r, item):
-        _, away = parts(item)
-
-        @pl.when(away == 0)
-        def _():
-            for side in range(2):
+        @pl.when(away(item) == 0)
+        def _():
+            for side in range(3):
                 to_owner(r, item, side).wait_recv()
 
     def sent(r, item):
-        _, away = parts(item)
-
-        @pl.when(away != 0)
+        @pl.when(away(item) != 0)
         def _():
             to_owner(r, item, 0).wait_send()
 
     def own_items(halves):
         def run(act):
             for i in (0, 2):
-                act((halves, (i, 2), BLOCK, x, i, i // 2))
+                act((halves, (i, 2), BLOCK, x, i))
 
         return run
 
@@ -240,7 +236,7 @@
             def _(d):
                 for pair in range(low, low + 4 if n == 2 else low + 1, n):
                     zd = (x + 3 - 2 * d + d // 2) % 4
-                    act((halves, (slot_of(pair, d), n), BLOCK, zd, pair + 4 * (d // 2), pair // 2))
+                    act((halves, (slot_of(pair, d), n), BLOCK, zd, pair + 4 * (d // 2)))
 
         return run
 
@@ -249,16 +245,16 @@
             @pl.loop(0, 2)
             def _(d):
                 if pair < 6:
-                    act((halves, (slot_of(pair, d), 1), BLOCK, (x + 2) % 4, pair - 4 + 2 * d, pair % 2))
+                    act((halves, (slot_of(pair, d), 1), BLOCK, (x + 2) % 4, pair - 4 + 2 * d))
                 else:
-                    act((halves, (slot_of(pair, d), 1), BLOCK, (x + 3 - 2 * d + 4) % 4, pair - 1, pair % 2))
+                    act((halves, (slot_of(pair, d), 1), BLOCK, (x + 3 - 2 * d + 4) % 4, pair - 1))
 
             if pair == 4:
-                act((halves, (26, 1), PIECE, (x + 3) % 4, 4, 0))
-                act((halves, (31, 1), PIECE, (x + 1) % 4, 4, 1))
+                act((halves, (26, 1), PIECE, (x + 3) % 4, 4))
+                act((halves, (31, 1), PIECE, (x + 1) % 4, 4))
             else:
                 q = (4, 6, 5, 7)[pair - 5]
-                act((halves, (slot_of(pair, 2), 1), BLOCK, (x + 2) % 4, q, (pair + 1) % 2))
+                act((halves, (slot_of(pair, 2), 1), BLOCK, (x + 2) % 4, q))
 
         return run
 
@@ -266,11 +262,10 @@
         def run(act):
             @pl.loop(0, 2)
             def _(d):
-                act((halves, (32 + d, 1), PIECE, (x + 3 - 2 * d) % 4, 8, 1))
+                act((halves, (32 + d, 1), PIECE, (x + 3 - 2 * d) % 4, 8))
 
         return run
 
-    waiting = [[], []]
     gone = [[], []]
 
     def over(r, items, act):
@@ -279,16 +274,9 @@
             for run in items:
                 run(lambda item: act(r, item))
 
-    def relay():
-        for r in range(2):
-            if waiting[r]:
-                over(r, waiting[r], pass_on)
-                gone[r] += waiting[r]
-                waiting[r] = []
-
-    def collect(r, items):
+    def collect(r, items, pair=0):
         over(r, items, add_up)
-        waiting[r] += items
+        gone[r] += [(run, pair) for run in items]
 
     wct[...] = jnp.zeros_like(wct)
     wct[0:4, :] = wcown[...]
@@ -300,7 +288,6 @@
         part = pl.ds(pl.multiple_of(i * 128, 128), 128)
         wck[part, :] = wct[:, part].astype(f32).T.astype(bf16)
 
-    both, first, second = (0, 2), (0, 1), (1, 1)
     compute(0, own_slots, 2)
     collect(0, [own_items(both)])
 
@@ -333,7 +320,7 @@
         lane = lax.broadcasted_iota(jnp.int32, (n, 128), 1)
         marks = jnp.zeros((n, 128), f32)
         for half in range(2):
-            full = zr[0, half, q, 0:n, :] + (zr[1, half, q, 0:n, :] + zr[2, half, q, 0:n, :])
+            full = (zr[0, half, q, 0:n, :] + zr[1, half, q, 0:n, :]) + (zr[2, half, q, 0:n, :] + zr[3, half, q, 0:n, :])
             obuf[pl.ds(pl.multiple_of(row, PIECE), n), 256 * half : 256 * (half + 1)] = full.astype(bf16)
             colsum[:, 256 * half : 256 * (half + 1)] += full.reshape(n // 8, 8, 256).sum(0)
             for b in range(2):
@@ -349,7 +336,9 @@
         def _():
             far.start()
 
-        check = zr[0, 0, q, n : n + 8, 0:n] + (zr[1, 0, q, n : n + 8, 0:n] + zr[2, 0, q, n : n + 8, 0:n])
+        check = (zr[0, 0, q, n : n + 8, 0:n] + zr[1, 0, q, n : n + 8, 0:n]) + (
+            zr[2, 0, q, n : n + 8, 0:n] + zr[3, 0, q, n : n + 8, 0:n]
+        )
         rrbuf[q, :, 0:n] = (check - marks.T[0:8]) * CHECK_BLOCK ** (-0.5)
 
     row_own = (y % 2) * 256
@@ -376,51 +365,60 @@
         def _(q):
             act(q, row_own + BLOCK * q, BLOCK)
 
-    def catch_up(pairs, half):
-        w_copy[half].wait_recv()
-        mm(0, own_slots, 2 + half)
-        for low, high in pairs:
-            if high - low == 1:
-                mm(row_of(2 * low, 0), pair_slots(low), 2 + half)
-            else:
-
-                @pl.loop(low, high)
-                def _(pair):
-                    mm(PIECE * OWN + 192 * pair, pair_slots(pair), 2 + half)
+    def early_mm(one):
+        one(0, own_slots)
+
+        @pl.loop(0, 4)
+        def _(pair):
+            one(PIECE * OWN + 192 * pair, pair_slots(pair))
+
+    def late_mm(one, low, high):
+        for pair in range(low, min(high, 5)):
+            one(row_of(2 * pair, 0), pair_slots(pair))
+        if high > 5:
+
+            @pl.loop(max(low, 5), high)
+            def _(pair):
+                one(PIECE * OWN + 192 * pair, pair_slots(pair))
 
     for pair in range(9):
         arrive(2 * pair)
         arrive(2 * pair + 1)
-        relay()
-        compute(row_of(2 * pair, 0), pair_slots(pair), 2 if pair < 4 else 3 if pair < 8 else 4)
+        row, slots = row_of(2 * pair, 0), pair_slots(pair)
+        compute(row, slots, 2 if pair < 4 else 3 if pair < 8 else 4)
         if pair < 4:
-            if pair == 3:
-                catch_up([(0, 4)], 0)
             collect(0, [early_items(both, pair, 1)])
-            if pair == 3:
-                collect(1, [own_items(first), early_items(first, 0, 2)])
         else:
-            if pair == 7:
-                catch_up([(0, 4), (4, 5), (5, 8)], 1)
-            collect(0, [late_items(both, pair)])
-            collect(1, [late_items(first if pair < 8 else both, pair)])
-            if pair == 7:
-                collect(1, [own_items(second), early_items(second, 0, 2)] + [late_items(second, k) for k in range(4, 8)])
-                relay()
-
-    early_gone = [list(items) for items in gone]
+            collect(0, [late_items(both, pair)], pair)
+            collect(1, [late_items(first if pair < 8 else both, pair)], pair)
+        if pair == 3:
+            w_copy[0].wait_recv()
+            early_mm(lambda row, slots: mm(row, slots, 2))
+            collect(1, [own_items(first), early_items(first, 0, 2)])
+        for at, part in ((5, third), (7, fourth)):
+            if pair == at:
+                w_copy[part[-1]].wait_recv()
+                early_mm(lambda row, slots: mm_part(row, slots, part))
+                collect(1, [own_items(part), early_items(part, 0, 2)])
+                late_mm(lambda row, slots: mm_part(row, slots, part), 4, pair + 1)
+                collect(1, [late_items(part, k) for k in range(4, pair + 1)])
+            elif at < pair < 8 and part == third:
+                mm_part(row, slots, part)
+                collect(1, [late_items(part, pair)])
+    early_gone = [[run for run, pair in gone[r] if pair < 8] for r in range(2)]
+    late_gone = [[run for run, pair in gone[r] if pair == 8] for r in range(2)]
+
+    arrive(18)
+    compute(row_of(18, 0), last_slots, 4)
+    for r in range(2):
+        collect(r, [last_items(both)], 8)
+        late_gone[r].append(last_items(both))
     for r in range(2):
         over(r, early_gone[r], take)
     finish_own(finish)
     finish_near(finish, False)
-    relay()
-    arrive(18)
-    compute(row_of(18, 0), last_slots, 4)
     for r in range(2):
-        collect(r, [last_items(both)])
-    relay()
-    for r in range(2):
-        over(r, gone[r][len(early_gone[r]) :], take)
+        over(r, late_gone[r], take)
     finish_near(finish, True)
 
     near_copies = [remote(colsum, nbuf.at[z], vs.at[d], vr.at[z], (dp, (t + d) % 8)) for d in range(1, 8)]
@@ -468,26 +466,39 @@
         for d in dirs(s):
             h_copy(s, d).wait_send()
     wc_copy.wait_send()
-    for j in range(2):
-        w_copy[j].wait_send()
+    for copy in w_copy:
+        copy.wait_send()
     for copy in check_copies:
         copy.wait_send()
-    def given(slot, n):
-        for half in range(2):
-            core_copy(half, slot, n + 8).wait_send()
-
-    @pl.loop(0, 26)
-    def _(slot):
-        given(slot, BLOCK)
-
-    @pl.loop(27, 31)
-    def _(slot):
-        given(slot, BLOCK)
-
-    for slot in (26, 31, 32, 33):
+    def given(slot, n, split=True):
+        core_copy(0, slot, n + 8).wait_send()
+        if not split:
+            core_copy(1, slot, n + 8).wait_send()
+            return
+
+        @pl.when(role == 1)
+        def _():
+            core_copy(1, slot, n + 8).wait_send()
+
+        @pl.when(role == 0)
+        def _():
+            for part in (third, fourth):
+                core_copy(1, slot, n, 3, part[2], part[3]).wait_send()
+
+    for low, high in ((0, 12), (13, 21), (22, 26), (27, 30)):
+
+        @pl.loop(low, high)
+        def _(slot):
+            given(slot, BLOCK)
+
+    for slot in (12, 21, 30):
+        given(slot, BLOCK, False)
+    for slot in (26, 31):
         given(slot, PIECE)
+    for slot in (32, 33):
+        given(slot, PIECE, False)
     for r in range(2):
-        over(r, gone[r], sent)
+        over(r, early_gone[r] + late_gone[r], sent)
 
     def written(side):
         def act(q, row, n):
@@ -570,8 +581,7 @@
             pltpu.VMEM((k, 128), bf16),
             pltpu.VMEM((4, SLOTS, BLOCK + 8, 256), f32),
             pltpu.VMEM((2, SLOTS, BLOCK + 8, 256), f32),
-            pltpu.VMEM((2, 2, 9, BLOCK + 8, 256), f32),
-            pltpu.VMEM((3, 2, 9, BLOCK + 8, 256), f32),
+            pltpu.VMEM((4, 2, 9, BLOCK + 8, 256), f32),
             pltpu.VMEM((512, 512), bf16),
             pltpu.VMEM((9, 8, 128), f32),
             pltpu.VMEM((2, 8, 256), f32),
@@ -585,13 +595,12 @@
             dma((9,)),
             dma((STEPS, 3)),
             dma((STEPS, 3)),
-            dma((3,)),
-            dma((3,)),
-            dma((2, SLOTS)),
-            dma((2, SLOTS)),
-            dma((2, SLOTS)),
-            dma((2, 2, 9)),
-            dma((2, 2, 9)),
+            dma((4,)),
+            dma((4,)),
+            dma((3, SLOTS)),
+            dma((3, SLOTS)),
+            dma((3, SLOTS)),
+            dma((3, 3, 9)),
             dma((9,)),
             dma((9,)),
             dma((1,)),

time: 142 us -> 137 us (0.965)
  Pallas kernels: 141 us -> 136 us
    pallas_call x1, Pallas kernels: 139 us -> 134 us  [shards(): pl.pallas_call(kernel, out_shape=shapes, in_specs=[whole] * 4, out_specs=...]
where the time goes in v4:
time: 137 us
  Pallas kernels  136 us (99%)
    pallas_call x1, Pallas kernels, shards(): pl.pallas_call(kernel, out_shape=shapes, in_specs=[whole] * 4, out_specs=...  134 us

profile of v4, /device:TPU:1, one launch (start us, length us, event | category | flops | bytes accessed | tf_op | source)
XLA Modules:
  0.0 136.7 jit_solution(12155681375324797698)
XLA Ops:
  0.6 134.2 %shard_map.67 = (bf16[512,512]{1,0:T(8,128)(2,1)}, f32[4,512]{1,0:T(4,128)}, f32[1,512]{1,0:T(1,128)}) custom-call(bf16[256,3584]{1,0:T(8,128)(2,1)} %h_hbm.1, bf16[16,3584]{1,0:T(8,128)(2,1)} %hc_hbm.1, bf16[3584,512]{1,0:T(8,128)(2,1)} %w_hbm.1, bf16[4,3584]{1,0:T(4,128)(2,1)} %bitcast.3), custom_call_target="tpu_custom_call" | custom-call | tf_op jit(solution)/shard_map/pallas_call | solution.py:569
  134.8 1.9 %shard_map.68 = (bf16[512,512]{1,0:T(8,128)(2,1)}, f32[4,512]{1,0:T(4,128)}, f32[1,512]{1,0:T(1,128)}) custom-call(bf16[512,512]{1,0:T(8,128)(2,1)} %get-tuple-element.9.out_in, f32[4,512]{1,0:T(4,128)} %get-tuple-element.10.rr_in, f32[1,512]{1,0:T(1,128)} %get-tuple-element.11.col_in), custom_call_target="tpu_custom_call" | custom-call | tf_op jit(solution)/shard_map/pallas_call | solution.py:617

commit v5 on v4

--- a/solution.py
+++ b/solution.py
@@ -11,7 +11,7 @@
 PIECE = 32
 OWN = 8
 STEPS = 19
-AHEAD = 4
+AHEAD = 3
 BLOCK = 64
 SLOTS = 34
 
@@ -92,7 +92,7 @@
         )
 
     h_in.wait()
-    for s in range(OWN):
+    for s in range(AHEAD):
         for d in dirs(s):
             h_copy(s, d).start()
     wc_in.wait()
@@ -305,9 +305,9 @@
     def arrive(s):
         for d in dirs(s):
             h_copy(s, d).wait_recv()
-        for later in range(OWN, STEPS):
+        for later in range(AHEAD, STEPS):
             for d in dirs(later):
-                if max(later - AHEAD, source(later, d)[0]) == s:
+                if max(later - AHEAD, source(later, d)[0] or 0) == s:
                     h_copy(later, d).start()
 
     def out_copies(q, row, n):

time: 137 us -> 132 us (0.964)
  Pallas kernels: 136 us -> 131 us
    pallas_call x1, Pallas kernels: 134 us -> 129 us  [shards(): pl.pallas_call(kernel, out_shape=shapes, in_specs=[whole] * 4, out_specs=...]
where the time goes in v5:
time: 132 us
  Pallas kernels  131 us (99%)
    pallas_call x1, Pallas kernels, shards(): pl.pallas_call(kernel, out_shape=shapes, in_specs=[whole] * 4, out_specs=...  129 us

profile of v5, /device:TPU:1, one launch (start us, length us, event | category | flops | bytes accessed | tf_op | source)
XLA Modules:
  0.0 131.7 jit_solution(4493251639723228247)
XLA Ops:
  0.6 129.1 %shard_map.67 = (bf16[512,512]{1,0:T(8,128)(2,1)}, f32[4,512]{1,0:T(4,128)}, f32[1,512]{1,0:T(1,128)}) custom-call(bf16[256,3584]{1,0:T(8,128)(2,1)} %h_hbm.1, bf16[16,3584]{1,0:T(8,128)(2,1)} %hc_hbm.1, bf16[3584,512]{1,0:T(8,128)(2,1)} %w_hbm.1, bf16[4,3584]{1,0:T(4,128)(2,1)} %bitcast.3), custom_call_target="tpu_custom_call" | custom-call | tf_op jit(solution)/shard_map/pallas_call | solution.py:569
  129.8 1.9 %shard_map.68 = (bf16[512,512]{1,0:T(8,128)(2,1)}, f32[4,512]{1,0:T(4,128)}, f32[1,512]{1,0:T(1,128)}) custom-call(bf16[512,512]{1,0:T(8,128)(2,1)} %get-tuple-element.9.out_in, f32[4,512]{1,0:T(4,128)} %get-tuple-element.10.rr_in, f32[1,512]{1,0:T(1,128)} %get-tuple-element.11.col_in), custom_call_target="tpu_custom_call" | custom-call | tf_op jit(solution)/shard_map/pallas_call | solution.py:617
